TPU v7x, 32 devices: a whole 2x2x4 slice. The times are simulated.
32 devices in a mesh: gx: 2 (over y), gy: 8 (over z, core), gz: 2 (over x).
Axes of the slice: x: 2, y: 2, z: 4, core: 2. Of those that a mesh axis runs over, the one named last changes fastest.
Arguments:
- starting_kelvin: float32 [16, 32, 2048], P(None, 'gx', ('gy', 'gz')), may hold values from -6 to 6
- substance_label: int32 [16, 32, 2048], P(None, 'gx', ('gy', 'gz')), may hold values from 0 to 3
- voxel_source_patch: int32 [16, 32, 2048], P(None, 'gx', ('gy', 'gz')), may hold values from 0 to 15
- substance_traits: float32 [4, 4], replicated, may hold values from 0.5 to 2
- patch_source_intensity: float32 [16], replicated, may hold values from 0 to 8
Outputs:
- warmed_result: float32 [16, 32, 2048], P(None, 'gx', ('gy', 'gz'))
- solution: float32 [3, 16, 32, 2048], P(None, 'gz', 'gx', 'gy')
- residual: float32 [3, 16, 32, 2048], P(None, 'gz', 'gx', 'gy')
All inputs are finite; a program needn't handle non-finite values.
Results may differ from a plain program's by a relative error of at most 0.0029.
Values sent between devices are 32-bit elements; how exact they have to be, the bound alone decides.
A program may use at most 64 MiB of HBM per device.

v0:
```python
import functools

import jax
import jax.numpy as jnp
from jax import lax
from jax.experimental import pallas as pl
from jax.experimental.pallas import tpu as pltpu
from jax.sharding import PartitionSpec as P

ITERS = 3
HALO = 8
REACH = 6
EDGE = 4
TIME_STEP = 0.03
ANCHOR = 0.5
K_TOTAL = 4 * 0.25 + 4 * 0.125 + 2 * (0.75 + 4 * 0.25 + 4 * 5.0 / 36.0)
MESH = pl.DeviceIdType.MESH
DIRECTIONS = [(dx, dc) for dx in (-1, 0, 1) for dc in (-1, 0, 1) if (dx, dc) != (0, 0)]


def shift(f, axis, step):
    return pltpu.roll(f, (-step) % f.shape[axis], axis)


def sums(f, axis):
    after, before = shift(f, axis, 1), shift(f, axis, -1)
    return after + before, after - before


def matrix_parts(f, width=None):
    sy, dy = sums(f, 1)
    if width is not None:
        f, sy, dy = f[:, :width], sy[:, :width], dy[:, :width]
    sx, dx = sums(f, 0)
    sxsy, dxsy = sums(sy, 0)
    sxdy, dxdy = sums(dy, 0)
    return sx, sy, sxsy, dx * 0.125 + dxsy * (1.0 / 18.0), dy * 0.125 + sxdy * (1.0 / 18.0), dxdy


def diag_z(f, sx, sy, sxsy):
    near = 0.25 * (sx + sy)
    return near + 0.125 * sxsy, 0.75 * f + near + (5.0 / 36.0) * sxsy


def diag_x(f, sx, sy, sxsy):
    near = 0.25 * sy
    return 0.75 * sx + near + 0.25 * sxsy, 0.25 * (f + sx) + 0.125 * sy + (5.0 / 36.0) * sxsy


def diag_y(f, sx, sy, sxsy):
    near = 0.25 * sx
    return 0.75 * sy + near + 0.25 * sxsy, 0.25 * (f + sy) + 0.125 * sx + (5.0 / 36.0) * sxsy


def vector_stencil(uz, ux, uy, width):
    sx, sy, sxsy, ex, ey, _ = matrix_parts(uz, width)
    uz, ux_in, uy_in = uz[:, :width], ux[:, :width], uy[:, :width]
    z0, z1 = diag_z(uz, sx, sy, sxsy)
    dif_x, dif_y = ex, ey
    sx, sy, sxsy, ex, _, cross_x = matrix_parts(ux, width)
    x0, x1 = diag_x(ux_in, sx, sy, sxsy)
    dif_z = ex
    sx, sy, sxsy, _, ey, cross_y = matrix_parts(uy, width)
    y0, y1 = diag_y(uy_in, sx, sy, sxsy)
    dif_z = dif_z + ey
    x0, x1 = x0 + 0.125 * cross_y, x1 + (1.0 / 18.0) * cross_y
    y0, y1 = y0 + 0.125 * cross_x, y1 + (1.0 / 18.0) * cross_x
    return (z0, x0, y0), (z1, x1, y1), (dif_z, dif_x, dif_y)


def gradient_stencil(f):
    sy, dy = sums(f, 1)
    sx, dx = sums(f, 0)
    sxsy, dxsy = sums(sy, 0)
    sxdy, _ = sums(dy, 0)
    zero = jnp.zeros_like(f)
    return (
        (zero, 0.5 * dx + 0.25 * dxsy, 0.5 * dy + 0.25 * sxdy),
        (zero, 0.25 * dx + (1.0 / 6.0) * dxsy, 0.25 * dy + (1.0 / 6.0) * sxdy),
        (0.5 * f + 0.25 * (sx + sy) + (1.0 / 6.0) * sxsy, zero, zero),
    )


def stream(layers, count, zero, planes, emit, extra):
    def body(p, carry):
        held, below, extra = carry
        same, both, diff = planes(p)
        out = [h + b + d for h, b, d in zip(held, both, diff)]
        extra = emit(p - 1, out, extra)
        held = [w + s for w, s in zip(below, same)]
        below = [b - d for b, d in zip(both, diff)]
        return held, below, extra

    zeros = [zero] * count
    return lax.fori_loop(1, layers + 2, body, (zeros, list(zeros), extra), unroll=4)[2]


def kernel(
    sizes,
    kelvin, label, patch, traits_in, power_in,
    warmed_out, solution_out, residual_out,
    traits, power_table, table_sem, warmed, solution, residual, vown, moment_s, out_sem,
    temp, temp2, lab, pat, cond, mod, strain, mask, gx_s, gy_s, gz_s, rate_s, pow_s, mats,
    v, vrecv, pack_f, pack_i, got_f, got_i, red_src, red_buf,
    local_sem, send_sem, recv_sem, vsend_sem, vrecv_sem, rsend_sem, rrecv_sem,
):
    nx, ny, nz = sizes
    nc, total = ny * nz, nx * ny * nz
    layers, rows, cols = kelvin.shape
    share = layers // nz
    full_rows = rows + 2 * HALO
    shape = (full_rows, 2 * cols)
    kept = slice(HALO - EDGE, HALO + rows + EDGE)
    inner_rows = slice(EDGE, EDGE + rows)
    ix, iy, iz = lax.axis_index("gx"), lax.axis_index("gy"), lax.axis_index("gz")
    ic = iy * nz + iz
    me = ix * nc + ic

    def coords(flat):
        return (flat // nc, (flat % nc) // nz, flat % nz)

    barrier = pltpu.get_barrier_semaphore()

    def greet(k, _):
        pl.semaphore_signal(
            barrier, inc=1, device_id=coords(lax.rem(me + k, total)), device_id_type=MESH
        )
        return 0

    lax.fori_loop(1, total, greet, 0, unroll=4)

    own = (slice(None), pl.ds(HALO, rows), pl.ds(0, cols))
    local = [
        pltpu.make_async_copy(a, b.at[own], local_sem.at[i])
        for i, (a, b) in enumerate(((kelvin, temp), (label, lab), (patch, pat)))
    ]
    tables = [
        pltpu.make_async_copy(traits_in, traits, table_sem.at[0]),
        pltpu.make_async_copy(power_in, power_table, table_sem.at[1]),
    ]
    for copy in local + tables:
        copy.start()

    sources = (kelvin, label, patch)
    pl.semaphore_wait(barrier, total - 1)

    def transfers(number):
        dx, dc = DIRECTIONS[number]
        there = (lax.rem(ix + dx + nx, nx) * nc) + lax.rem(ic + dc + nc, nc)
        target = jnp.logical_and(
            jnp.logical_and(ix + dx >= 0, ix + dx < nx), jnp.logical_and(ic + dc >= 0, ic + dc < nc)
        )
        origin = jnp.logical_and(
            jnp.logical_and(ix - dx >= 0, ix - dx < nx), jnp.logical_and(ic - dc >= 0, ic - dc < nc)
        )
        if dx == 0:
            from_rows, to_rows = pl.ds(0, rows), pl.ds(HALO, rows)
        elif dx == 1:
            from_rows, to_rows = pl.ds(rows - REACH, REACH), pl.ds(HALO - REACH, REACH)
        else:
            from_rows, to_rows = pl.ds(0, REACH), pl.ds(HALO + rows, REACH)
        if dc == 0:
            pairs = [
                (ref.at[:, from_rows, :], ext.at[:, to_rows, pl.ds(0, cols)])
                for ref, ext in zip(sources, (temp, lab, pat))
            ]
        else:
            side = (dc + 1) // 2
            pairs = [(pack_f.at[side, from_rows, :], got_f.at[side, to_rows, :])]
            pairs += [
                (pack_i.at[side, i, from_rows, :], got_i.at[side, i, to_rows, :]) for i in (0, 1)
            ]
        copies = [
            pltpu.make_async_remote_copy(
                src_ref=a, dst_ref=b, send_sem=send_sem.at[number, i],
                recv_sem=recv_sem.at[number, i], device_id=coords(there), device_id_type=MESH,
            )
            for i, (a, b) in enumerate(pairs)
        ]
        return target, origin, copies, to_rows, dc

    moves = [transfers(i) for i in range(len(DIRECTIONS))]
    for target, _, copies, _, dc in moves:
        if dc != 0:
            continue

        @pl.when(target)
        def _(copies=copies):
            for copy in copies:
                copy.start()

    lane = lax.broadcasted_iota(jnp.int32, (rows, cols), 1)
    for copy in local:
        copy.wait()
    for side in (0, 1):
        for index, ref in enumerate((temp, lab, pat)):
            packed = jnp.zeros((rows, cols), ref.dtype)
            for z in range(layers):
                amount = (HALO * z + (HALO if side else 0)) % cols
                piece = ref[(z, *own[1:])]
                piece = pltpu.roll(piece, amount, 1) if amount else piece
                packed = jnp.where(lane // HALO == z, piece, packed)
            if index == 0:
                pack_f[side] = packed
            else:
                pack_i[side, index - 1] = packed

    for target, _, copies, _, dc in moves:
        if dc == 0:
            continue

        @pl.when(target)
        def _(copies=copies):
            for copy in copies:
                copy.start()

    for _, origin, _, to_rows, dc in moves:
        @pl.when(jnp.logical_not(origin))
        def _(to_rows=to_rows, dc=dc):
            if dc == 0:
                block = (layers, to_rows.size, cols)
                temp[:, to_rows, 0:cols] = jnp.zeros(block, jnp.float32)
                lab[:, to_rows, 0:cols] = jnp.full(block, -1, jnp.int32)
                pat[:, to_rows, 0:cols] = jnp.zeros(block, jnp.int32)
            else:
                side = (dc + 1) // 2
                block = (to_rows.size, cols)
                got_f[side, to_rows, :] = jnp.zeros(block, jnp.float32)
                got_i[side, 0, to_rows, :] = jnp.full(block, -1, jnp.int32)
                got_i[side, 1, to_rows, :] = jnp.zeros(block, jnp.int32)

    empty = jnp.zeros(shape, jnp.float32)
    blank_kept = jnp.zeros((rows + 2 * EDGE, 2 * cols), jnp.float32)
    for end in (0, layers + 1):
        for ref in (mod, strain, mask):
            ref[end] = blank_kept
        for k in range(ITERS):
            for c in range(3):
                v[k, c, end] = blank_kept
    for c in range(6):
        mats[c, 0] = blank_kept
    cond[layers] = empty

    for copy in tables:
        copy.wait()
    shift_scalar = 3.0 * (traits[2, 0] + traits[2, 1] + traits[2, 2] + traits[2, 3])
    inverse_shift = 1.0 / jnp.full((1, 2 * cols), shift_scalar, jnp.float32)

    for _, origin, copies, _, _ in moves:
        @pl.when(origin)
        def _(copies=copies):
            for copy in copies:
                copy.wait_recv()

    halo_lane = lax.broadcasted_iota(jnp.int32, (full_rows, cols), 1)
    materials = traits.shape[1]
    tiles = power_table.shape[0]

    def prepare(z, _):
        def unpack(left, right, outside):
            left = pltpu.roll(left, lax.rem(2 * cols - HALO - HALO * z, cols), 1)
            right = pltpu.roll(right, lax.rem(cols - HALO * z, cols), 1)
            rest = jnp.where(halo_lane >= cols - HALO, left, outside)
            return jnp.where(halo_lane < HALO, right, rest)

        temp[z, :, cols:] = unpack(got_f[1], got_f[0], jnp.float32(0.0))
        label_halo = unpack(got_i[1, 0], got_i[0, 0], jnp.int32(-1))
        patch_halo = unpack(got_i[1, 1], got_i[0, 1], jnp.int32(0))
        for part, ids, patches in (
            (pl.ds(0, cols), lab[z, :, 0:cols], pat[z, :, 0:cols]),
            (pl.ds(cols, cols), label_halo, patch_halo),
        ):
            near = ids[kept]
            values = [jnp.zeros(a.shape, jnp.float32) for a in (ids, ids, near, near)]
            for m in range(materials):
                hit, near_hit = ids == m, near == m
                hits = (hit, hit, near_hit, near_hit)
                values = [jnp.where(hits[q], traits[q, m], values[q]) for q in range(4)]
            inside = ids >= 0
            cond[z, :, part] = values[0]
            rate_s[z, :, part] = jnp.where(inside, TIME_STEP / jnp.where(inside, values[1], 1.0), 0.0)
            mod[z + 1, :, part] = values[2] * inverse_shift[:, 0:cols]
            strain[z + 1, :, part] = values[3]
            mask[z + 1, :, part] = jnp.where(near >= 0, 1.0, 0.0)
            power = jnp.zeros(ids.shape, jnp.float32)
            for t in range(tiles):
                power = jnp.where(patches == t, power_table[t], power)
            pow_s[z, :, part] = power
        return 0

    lax.fori_loop(0, layers, prepare, 0, unroll=4)

    def conduct(a, b):
        return 2.0 * a * b / jnp.maximum(a + b, 0.25)

    def heat(z, flow_below, source, first):
        centre = source[z]
        if first:
            own_cond = cond[z]
            along_x = conduct(own_cond, shift(own_cond, 0, 1))
            along_y = conduct(own_cond, shift(own_cond, 1, 1))
            along_z = conduct(own_cond, cond[z + 1])
            gx_s[z], gy_s[z], gz_s[z] = along_x, along_y, along_z
        else:
            along_x, along_y, along_z = gx_s[z], gy_s[z], gz_s[z]
        flow_x = along_x * (shift(centre, 0, 1) - centre)
        flow_y = along_y * (shift(centre, 1, 1) - centre)
        flow_z = along_z * (source[jnp.minimum(z + 1, layers - 1)] - centre)
        flux = flow_x - shift(flow_x, 0, -1) + flow_y - shift(flow_y, 1, -1) + flow_z - flow_below
        return centre + rate_s[z] * (flux + pow_s[z]), flow_z

    def first_step(z, flow_below):
        temp2[z], flow_z = heat(z, flow_below, temp, True)
        return flow_z

    blank = mod[0]
    lax.fori_loop(0, layers, first_step, cond[layers], unroll=4)

    def second_step(z, flow_below):
        value, flow_z = heat(z, flow_below, temp2, False)
        warmed[z] = value[HALO : HALO + rows, 0:cols]
        strain[z + 1] = strain[z + 1] * value[kept]
        return flow_z

    lax.fori_loop(0, layers, second_step, cond[layers], unroll=4)
    results = [pltpu.make_async_copy(warmed, warmed_out, out_sem.at[0])]
    results[0].start()


    def matrix_planes(p):
        f = mod[p]
        sx, sy, sxsy, ex, ey, cross = matrix_parts(f)
        z0, z1 = diag_z(f, sx, sy, sxsy)
        x0, x1 = diag_x(f, sx, sy, sxsy)
        y0, y1 = diag_y(f, sx, sy, sxsy)
        zero = jnp.zeros_like(f)
        return (
            (z0, x0, y0, zero, zero, 0.125 * cross),
            (z1, x1, y1, zero, zero, (1.0 / 18.0) * cross),
            (zero, zero, zero, ex, ey, zero),
        )

    def matrix_emit(p, out, extra):
        diagonal = (ANCHOR + K_TOTAL) * mod[p] - 1.0
        for c in range(6):
            mats[c, p] = out[c] + diagonal if c < 3 else out[c]
        return extra

    stream(layers, 6, blank, matrix_planes, matrix_emit, 0)

    def fold(inner):
        result = inner[0:8]
        for r in range(8, rows, 8):
            result = result + inner[r : r + 8]
        return result

    tile = mod[0, 0:8, 0:cols]

    def load_planes(p):
        m, s = mod[p], strain[p]
        parts = [gradient_stencil(f) for f in (s, m, m * s)]
        return tuple(tuple(a for part in parts for a in part[i]) for i in range(3))

    def load_emit(p, out, acc):
        m, s, inside = mod[p], strain[p], mask[p]
        for c in range(3):
            value = -inside * (m * out[c] + s * out[3 + c] + out[6 + c])
            v[0, c, p] = value
            inner = value[inner_rows, 0:cols]
            vown[0, c, p] = inner
            acc = acc + fold(inner * inner)
        return acc

    moment_s[0] = stream(layers, 9, blank, load_planes, load_emit, tile)

    def shares(k):
        found = []
        for step in range(1, nz):
            there = lax.rem(iz + step, nz)
            found.append(
                pltpu.make_async_remote_copy(
                    src_ref=vown.at[k, :, pl.ds(1 + there * share, share)],
                    dst_ref=vrecv.at[k, step - 1],
                    send_sem=vsend_sem.at[k, step - 1], recv_sem=vrecv_sem.at[k, step - 1],
                    device_id=(ix, iy, there), device_id_type=MESH,
                )
            )
        return found

    def share_basis(k):
        for copy in shares(k):
            copy.start()

    share_basis(0)

    def apply(k, width):
        def planes(p):
            m = mod[p]
            u = [v[k, c, p] for c in range(3)]
            first = vector_stencil(*u, width)
            second = vector_stencil(*[m * f for f in u], width)
            return tuple(a + b for a, b in zip(first, second))

        def emit(p, out, acc):
            m = mod[p, :, 0:width]
            u = [v[k, c, p, :, 0:width] for c in range(3)]
            zz, xx, yy, zx, zy, xy = [mats[c, p, :, 0:width] for c in range(6)]
            grown = (
                zz * u[0] + zx * u[1] + zy * u[2],
                zx * u[0] + xx * u[1] + xy * u[2],
                zy * u[0] + xy * u[1] + yy * u[2],
            )
            odd, even = acc
            for c in range(3):
                value = grown[c] - m * out[c] - out[3 + c]
                if width > cols:
                    value = mask[p] * value
                    v[k + 1, c, p] = value
                inner = value[inner_rows, 0:cols]
                vown[k + 1, c, p] = inner
                odd = odd + fold(inner * vown[k, c, p])
                even = even + fold(inner * inner)
            return odd, even

        odd, even = stream(layers, 6, mod[0, :, 0:width], planes, emit, (tile, tile))
        moment_s[2 * k + 1] = odd
        moment_s[2 * k + 2] = even

    def grow(k, _):
        apply(k, 2 * cols)
        share_basis(k + 1)
        return 0

    lax.fori_loop(0, ITERS - 1, grow, 0)
    apply(ITERS - 1, cols)

    lane8 = lax.broadcasted_iota(jnp.int32, (1, cols), 1)
    row = jnp.zeros((1, cols), jnp.float32)
    for k in range(2 * ITERS):
        line = jnp.sum(moment_s[k], axis=0, keepdims=True)
        row = jnp.where(lane8 == k, jnp.sum(line, axis=1, keepdims=True), row)
    red_src[...] = row
    red_buf[me] = row

    def spread(k):
        there = lax.rem(me + k, total)
        return pltpu.make_async_remote_copy(
            src_ref=red_src, dst_ref=red_buf.at[me], send_sem=rsend_sem.at[k],
            recv_sem=rrecv_sem.at[k], device_id=coords(there), device_id_type=MESH,
        )

    def collect(k):
        there = lax.rem(me + total - k, total)
        return pltpu.make_async_remote_copy(
            src_ref=red_src, dst_ref=red_buf.at[there], send_sem=rsend_sem.at[k],
            recv_sem=rrecv_sem.at[k], device_id=coords(there), device_id_type=MESH,
        )

    def start(k, _):
        spread(k).start()
        return 0

    def finish(k, _):
        collect(k).wait_recv()
        return 0

    def sent(k, _):
        spread(k).wait_send()
        return 0

    lax.fori_loop(1, total, start, 0, unroll=4)
    share_basis(ITERS)
    lax.fori_loop(1, total, finish, 0, unroll=4)

    def add(k, acc):
        return acc + red_buf[k]

    summed = lax.fori_loop(0, total, add, jnp.zeros((1, cols), jnp.float32), unroll=4)
    m = [
        jnp.sum(jnp.where(lane8 == k, summed, 0.0), axis=1, keepdims=True) for k in range(2 * ITERS)
    ]

    def inner(a, b):
        value = None
        for i, x in enumerate(a):
            for j, y in enumerate(b):
                if x is not None and y is not None:
                    term = x * y * m[i + j]
                    value = term if value is None else value + term
        return value

    def plus(a, factor, b):
        out = []
        for x, y in zip(a, b):
            if y is None:
                out.append(x)
            else:
                out.append(factor * y if x is None else x + factor * y)
        return out

    one = jnp.ones((1, 1), jnp.float32)
    size = ITERS + 1
    res = [one] + [None] * ITERS
    dire = list(res)
    sol = [None] * size
    rr = m[0]
    for number in range(ITERS):
        image = plus(list(dire), 1.0, [None] + dire[:-1])
        alpha = rr / inner(dire, image)
        sol = plus(sol, alpha, dire)
        res = plus(res, -alpha, image)
        if number + 1 < ITERS:
            new = inner(res, res)
            dire = plus(res, new / rr, dire)
            rr = new
    res = [shift_scalar * x for x in res]

    for step in range(nz):
        where = pl.ds(pl.multiple_of(lax.rem(iz + nz - step, nz) * cols, cols), cols)
        for index, (weights, held, target) in enumerate(
            ((sol[:ITERS], solution, solution_out), (res, residual, residual_out))
        ):
            if step:
                for k in range(ITERS) if index == 0 else (ITERS,):
                    shares(k)[step - 1].wait_recv()

            def combine(z, _, step=step, weights=weights, held=held):
                for c in range(3):
                    value = None
                    for k, weight in enumerate(weights):
                        part = vown[k, c, 1 + iz * share + z] if step == 0 else vrecv[k, step - 1, c, z]
                        value = weight * part if value is None else value + weight * part
                    held[step, c, z] = value
                return 0

            lax.fori_loop(0, share, combine, 0, unroll=4)
            results.append(
                pltpu.make_async_copy(
                    held.at[step], target.at[:, :, :, where], out_sem.at[1 + 2 * step + index]
                )
            )
            results[-1].start()

    for target, _, copies, _, _ in moves:
        @pl.when(target)
        def _(copies=copies):
            for copy in copies:
                copy.wait_send()
    for k in range(ITERS + 1):
        for copy in shares(k):
            copy.wait_send()
    lax.fori_loop(1, total, sent, 0)
    for copy in results:
        copy.wait()


def per_device(sizes, *arrays):
    nx, ny, nz = sizes
    layers, rows, cols = arrays[0].shape
    total = nx * ny * nz
    share = layers // nz
    ext = (rows + 2 * HALO, 2 * cols)
    f32, i32 = jnp.float32, jnp.int32
    vmem = pltpu.VMEM
    dma = pltpu.SemaphoreType.DMA
    out = jax.ShapeDtypeStruct((3, share, rows, cols * nz), f32)
    plane = vmem((layers, *ext), f32)
    kept = (rows + 2 * EDGE, 2 * cols)
    padded = vmem((layers + 2, *kept), f32)
    half = vmem((nz, 3, share, rows, cols), f32)
    return pl.pallas_call(
        functools.partial(kernel, sizes),
        out_shape=(jax.ShapeDtypeStruct((layers, rows, cols), f32), out, out),
        in_specs=[pl.BlockSpec(memory_space=pltpu.HBM)] * 5,
        out_specs=[pl.BlockSpec(memory_space=pl.ANY)] * 3,
        scratch_shapes=[
            pltpu.SMEM(arrays[3].shape, f32), pltpu.SMEM(arrays[4].shape, f32), dma((2,)),
            vmem((layers, rows, cols), f32), half, half,
            vmem((ITERS + 1, 3, layers + 1, rows, cols), f32),
            vmem((2 * ITERS + 1, 8, cols), f32), dma((1 + 2 * nz,)),
            plane, plane, vmem((layers, *ext), i32), vmem((layers, *ext), i32),
            vmem((layers + 1, *ext), f32), padded, padded, padded,
            plane, plane, plane, plane, plane,
            vmem((6, layers + 1, *kept), f32),
            vmem((ITERS, 3, layers + 2, *kept), f32),
            vmem((ITERS + 1, nz - 1, 3, share, rows, cols), f32),
            vmem((2, rows, cols), f32), vmem((2, 2, rows, cols), i32),
            vmem((2, ext[0], cols), f32), vmem((2, 2, ext[0], cols), i32),
            vmem((1, cols), f32), vmem((total, 1, cols), f32),
            dma((3,)), dma((8, 3)), dma((8, 3)),
            dma((ITERS + 1, nz - 1)), dma((ITERS + 1, nz - 1)), dma((total,)), dma((total,)),
        ],
        compiler_params=pltpu.CompilerParams(
            collective_id=0, has_side_effects=True, vmem_limit_bytes=40 * 1024 * 1024
        ),
    )(*[pltpu.with_memory_space_constraint(a, pltpu.HBM) for a in arrays])


def solution(mesh):
    sizes = tuple(mesh.shape[axis] for axis in ("gx", "gy", "gz"))
    split = P(None, "gx", ("gy", "gz"))
    out = P(None, "gz", "gx", "gy")
    return jax.shard_map(
        functools.partial(per_device, sizes),
        mesh=mesh,
        in_specs=(split, split, split, P(), P()),
        out_specs=(split, out, out),
        check_vma=False,
    )
```

profile of v0, /device:TPU:0, one launch (start us, length us, event | category | flops | bytes accessed | tf_op | source)
XLA Modules:
  0.0 44.3 jit_solution(15771596513227893704)
XLA Ops:
  0.6 41.6 %shard_map.76 = (f32[16,16,128]{2,1,0:T(8,128)S(1)}, f32[3,8,16,256]{3,2,1,0:T(8,128)S(1)}, f32[3,8,16,256]{3,2,1,0:T(8,128)S(1)}) custom-call(f32[16,16,128]{2,1,0:T(8,128)} %kelvin.1, s32[16,16,128]{2,1,0:T(8,128)} %label.1, s32[16,16,128]{2,1,0:T(8,128)} %patch.1, f32[4,4]{1,0:T(4,128)} %traits_in.1, f32[16]{0:T(128)} %power_in.1), custom_call_target="tpu_custom_call" | custom-call | tf_op jit(solution)/shard_map/pallas_call | solution.py:571
  42.2 0.7 %copy.11 = f32[16,16,128]{2,1,0:T(8,128)} copy(f32[16,16,128]{2,1,0:T(8,128)S(1)} %get-tuple-element.6) | data formatting | bytes 262144
  42.9 0.7 %copy.12 = f32[3,8,16,256]{3,2,1,0:T(8,128)} copy(f32[3,8,16,256]{3,2,1,0:T(8,128)S(1)} %get-tuple-element.7) | data formatting | bytes 786432
  43.6 0.7 %copy.13 = f32[3,8,16,256]{3,2,1,0:T(8,128)} copy(f32[3,8,16,256]{3,2,1,0:T(8,128)S(1)} %get-tuple-element.8) | data formatting | bytes 786432
where the time goes:
time: 44.5 us; the launch traced here: 44.3 us
  Pallas kernels  41.6 us (93%)
  local copies, waits for them, and re-layouts  2.15 us (5%)
  between operations  0.64 us (1%)
    pallas_call x1, Pallas kernels, per_device(): pl.pallas_call(functools.partial(kernel, sizes), out_shape=(jax.ShapeDtyp...  41.6 us
    unnamed x3, local copies, waits for them, and re-layouts  2.15 us

commit v1 on v0

v1 whole, which is shorter than its diff:
```python
import functools

import jax
import jax.numpy as jnp
from jax import lax
from jax.experimental import pallas as pl
from jax.experimental.pallas import tpu as pltpu
from jax.sharding import PartitionSpec as P

ITERS = 3
HALO = 8
REACH = 6
EDGE = 4
STRIP = 16
PAIR = 2 * STRIP
TIME_STEP = 0.03
ANCHOR = 0.5
K_TOTAL = 4 * 0.25 + 4 * 0.125 + 2 * (0.75 + 4 * 0.25 + 4 * 5.0 / 36.0)
MESH = pl.DeviceIdType.MESH
DIRECTIONS = [(dx, dc) for dx in (-1, 0, 1) for dc in (-1, 0, 1) if (dx, dc) != (0, 0)]


def turn(f, amount):
    amount %= f.shape[-1]
    return pltpu.roll(f, amount, f.ndim - 1) if amount else f


def both_lanes(f):
    return turn(f, -1) + turn(f, 1)


def three(ref, index, at):
    low, mid, high = (ref[(*index, pl.ds(at + step, 8))] for step in (-1, 0, 1))
    return mid, high + low, high - low


def operator_parts(z, x, y):
    (pz, sz, dz), (px, sx, dx), (py, sy, dy) = z, x, y
    az, bz = pz + 0.5 * sz, pz + (5.0 / 9.0) * sz
    ay, by = py + 0.5 * sy, py + (5.0 / 9.0) * sy
    qx = px + sx
    half_dz, ninth_dz = 0.5 * dz, (2.0 / 9.0) * dz
    half_dx, ninth_dx = 0.5 * dx, (2.0 / 9.0) * dx
    half_dy, ninth_dy = 0.5 * dy, (2.0 / 9.0) * dy
    return (
        (2.0 * az + pz, sz, half_dx),
        (bz, az, ninth_dx),
        (None, None, ay - 0.5 * by),
        (qx, 3.0 * sx, half_dz),
        (0.5 * px + (5.0 / 9.0) * sx, qx, ninth_dz),
        (ninth_dy, half_dy, None),
        (ay, sy, None),
        (by, 2.0 * ay + py, None),
        (ninth_dx, half_dx, az - 0.5 * bz),
    )


def operator_finish(out):
    found = []
    for c in range(3):
        flat, even, odd = out[3 * c : 3 * c + 3]
        found.append(flat + turn(even + odd, -1) + turn(even - odd, 1))
    return found


def gradient_parts(f):
    p, s, d = f
    small = (2.0 / 3.0) * d
    return (
        (None, None, 2.0 * p + s),
        (None, None, p + (2.0 / 3.0) * s),
        (d, d + d, None),
        (small, d, None),
        (p + (2.0 / 3.0) * s, 2.0 * p + s, None),
    )


def gradient_finish(out):
    za, zb, xa, xb, yc = out
    return za + both_lanes(zb), xa + both_lanes(xb), turn(yc, -1) - turn(yc, 1)


def matrix_parts(f):
    p, s, d = f
    a, b = p + 0.5 * s, p + (5.0 / 9.0) * s
    q = p + s
    return (
        (2.0 * a + p, s, None), (b, a, None),
        (q, 3.0 * s, None), (0.5 * p + (5.0 / 9.0) * s, q, None),
        (a, s, None), (b, 2.0 * a + p, None),
        (None, None, 0.5 * d), (None, None, (2.0 / 9.0) * d),
        (None, None, a - 0.5 * b),
        ((2.0 / 9.0) * d, 0.5 * d, None),
    )


def matrix_finish(out):
    return (
        out[0] + both_lanes(out[1]), out[2] + both_lanes(out[3]), out[4] + both_lanes(out[5]),
        out[6] + both_lanes(out[7]), turn(out[8], -1) - turn(out[8], 1), turn(out[9], -1) - turn(out[9], 1),
    )


def absorb(parts, held, below):
    out, held_next, below_next = [], [], []
    for i, (side, centre, diff) in enumerate(parts):
        if side is None:
            up, down = diff, diff
            out.append(None if held is None else up - held[i])
            held_next.append(down if below is None else below[i])
            below_next.append(down)
            continue
        up = side if diff is None else side + diff
        down = side if diff is None else side - diff
        out.append(None if held is None else held[i] + up)
        held_next.append(centre if below is None else below[i] + centre)
        below_next.append(down)
    return out, held_next, below_next


def closing(kinds, held):
    return [-h if side is None else h for (side, _, _), h in zip(kinds, held)]


def stream_closed(first, count, parts, emit, unroll):
    kinds = parts(first)
    zero = jnp.zeros_like(next(c for _, c, _ in kinds if c is not None))
    held = [zero if side is None else centre for side, centre, _ in kinds]
    below = [
        diff if side is None else (side if diff is None else side - diff) for side, _, diff in kinds
    ]

    def body(p, carry):
        out, held, below = absorb(parts(p), *carry)
        emit(p - 1, out)
        return held, below

    held, below = lax.fori_loop(first + 1, first + count, body, (held, below), unroll=unroll)
    emit(first + count - 1, closing(kinds, held))


def stream_open(first, count, parts, emit):
    held = below = None
    for p in range(first - 1, first + count + 1):
        out, held_next, below = absorb(parts(p), held, below)
        if p > first:
            emit(p - 1, out)
        held = held_next if p >= first else None


def pick(bits, table, count):
    level = list(table)
    for bit in bits:
        level = [
            level[i] if i + 1 >= len(level) else jnp.where(bit, level[i + 1], level[i])
            for i in range(0, len(level), 2)
        ]
    return level[0]


def bits_of(ids, count):
    return [(ids & (1 << b)) != 0 for b in range(max(count - 1, 1).bit_length())]


def kernel(
    sizes,
    kelvin, label, patch, traits_in, power_in,
    warmed_out, solution_out, residual_out,
    traits, power_table, table_sem, warmed, solution, residual, vown, moment_s, out_sem,
    temp, temp2, lab, pat, cond, rate_s, pow_s, gx_s, gy_s, gz_s,
    mod, strain, both, mask, mats, v0, v1, v2, v3,
    vrecv, pack_f, pack_i, got_f, got_i, red_src, red_buf,
    local_sem, send_sem, recv_sem, vsend_sem, vrecv_sem, rsend_sem, rrecv_sem,
):
    nx, ny, nz = sizes
    v = (v0, v1, v2, v3)
    nc, total = ny * nz, nx * ny * nz
    layers, rows, cols = kelvin.shape
    share = layers // nz
    own_chunks = rows // 8
    chunks = own_chunks + 1
    heat_chunks = own_chunks + (1 if nx <= 2 else 2)
    groups = cols // PAIR
    tiles = layers // groups
    pads = (0, layers + 1)
    main = range(1, layers + 1)
    low_wrap, first_tile = layers + 2, layers + 3
    high_wrap = first_tile + tiles
    strips = range(first_tile, high_wrap)
    below_own, after_own = 8 + rows, 8 * heat_chunks
    ix, iy, iz = lax.axis_index("gx"), lax.axis_index("gy"), lax.axis_index("gz")
    ic = iy * nz + iz
    me = ix * nc + ic

    def at(chunk):
        return 8 + 8 * chunk

    def coords(flat):
        return (flat // nc, (flat % nc) // nz, flat % nz)

    for ref, fill in ((temp, 0), (lab, -1), (pat, 0)):
        for p in main:
            for chunk in range(own_chunks, heat_chunks):
                ref[p, at(chunk) : at(chunk) + 8] = jnp.full((8, cols), fill, ref.dtype)
    for side in (0, 1):
        for chunk in range(heat_chunks):
            where = slice(8 * chunk, 8 * chunk + 8)
            got_f[side, where] = jnp.zeros((8, cols), jnp.float32)
            got_i[side, 0, where] = jnp.full((8, cols), -1, jnp.int32)
            got_i[side, 1, where] = jnp.zeros((8, cols), jnp.int32)

    barrier = pltpu.get_barrier_semaphore()

    def greet(k, _):
        pl.semaphore_signal(
            barrier, inc=1, device_id=coords(lax.rem(me + k, total)), device_id_type=MESH
        )
        return 0

    lax.fori_loop(1, total, greet, 0, unroll=4)

    own = (slice(1, layers + 1), slice(8, 8 + rows))
    local = [
        pltpu.make_async_copy(a, b.at[own], local_sem.at[i])
        for i, (a, b) in enumerate(((kelvin, temp), (label, lab), (patch, pat)))
    ]
    tables = [
        pltpu.make_async_copy(traits_in, traits, table_sem.at[0]),
        pltpu.make_async_copy(power_in, power_table, table_sem.at[1]),
    ]
    for copy in local + tables:
        copy.start()

    raw = (temp, lab, pat)

    def transfers(number):
        dx, dc = DIRECTIONS[number]
        there = (lax.rem(ix + dx + nx, nx) * nc) + lax.rem(ic + dc + nc, nc)
        target = jnp.logical_and(
            jnp.logical_and(ix + dx >= 0, ix + dx < nx), jnp.logical_and(ic + dc >= 0, ic + dc < nc)
        )
        origin = jnp.logical_and(
            jnp.logical_and(ix - dx >= 0, ix - dx < nx), jnp.logical_and(ic - dc >= 0, ic - dc < nc)
        )
        if dx == 0:
            from_rows, to_rows = pl.ds(0, rows), pl.ds(0, rows)
        elif dx == 1:
            from_rows, to_rows = pl.ds(rows - REACH, REACH), pl.ds(8 * heat_chunks - REACH, REACH)
        else:
            from_rows, to_rows = pl.ds(0, REACH), pl.ds(rows, REACH)
        if dc == 0:
            source = pl.ds(8 + from_rows.start, from_rows.size)
            place = pl.ds(8 + to_rows.start, to_rows.size)
            pairs = [(ref.at[1 : layers + 1, source], ref.at[1 : layers + 1, place]) for ref in raw]
        else:
            side = (dc + 1) // 2
            pairs = [(pack_f.at[side, from_rows, :], got_f.at[side, to_rows, :])]
            pairs += [
                (pack_i.at[side, i, from_rows, :], got_i.at[side, i, to_rows, :]) for i in (0, 1)
            ]
        copies = [
            pltpu.make_async_remote_copy(
                src_ref=a, dst_ref=b, send_sem=send_sem.at[number, i],
                recv_sem=recv_sem.at[number, i], device_id=coords(there), device_id_type=MESH,
            )
            for i, (a, b) in enumerate(pairs)
        ]
        return target, origin, copies, dc

    moves = [transfers(i) for i in range(len(DIRECTIONS))]
    for copy in local:
        copy.wait()
    pl.semaphore_wait(barrier, total - 1)
    for target, _, copies, dc in moves:
        if dc != 0:
            continue

        @pl.when(target)
        def _(copies=copies):
            for copy in copies:
                copy.start()

    wide_lane = lax.broadcasted_iota(jnp.int32, (rows, cols), 1) // HALO
    for side in (0, 1):
        for index, ref in enumerate(raw):
            packed = jnp.zeros((rows, cols), ref.dtype)
            for z in range(layers):
                piece = turn(ref[(1 + z, own[1])], HALO * z + (HALO if side else 0))
                packed = jnp.where(wide_lane == z, piece, packed)
            if index == 0:
                pack_f[side] = packed
            else:
                pack_i[side, index - 1] = packed

    for target, _, copies, dc in moves:
        if dc == 0:
            continue

        @pl.when(target)
        def _(copies=copies):
            for copy in copies:
                copy.start()

    lane = lax.broadcasted_iota(jnp.int32, (8, cols), 1)
    row8 = lax.broadcasted_iota(jnp.int32, (8, cols), 0)
    empty = jnp.zeros((8, cols), jnp.float32)
    for p in pads:
        for chunk in range(heat_chunks):
            for ref in (temp, temp2, cond, gz_s):
                ref[p, at(chunk) : at(chunk) + 8] = empty

    for copy in tables:
        copy.wait()
    shift_scalar = 3.0 * (traits[2, 0] + traits[2, 1] + traits[2, 2] + traits[2, 3])
    quarter_inverse = 0.25 / jnp.full((8, cols), shift_scalar, jnp.float32)

    for _, origin, copies, _ in moves:
        @pl.when(origin)
        def _(copies=copies):
            for copy in copies:
                copy.wait_recv()

    group, spot = lane // PAIR, lane % PAIR
    for index, ref in enumerate(raw):
        def fill(chunk, _, index=index, ref=ref):
            pos = pl.multiple_of(8 * chunk, 8)
            here = pl.ds(pl.multiple_of(8 * chunk + 8, 8), 8)
            left, right = (
                got_f[side, pl.ds(pos, 8)] if index == 0 else got_i[side, index - 1, pl.ds(pos, 8)]
                for side in (1, 0)
            )
            for t in range(tiles):
                value = jnp.where(
                    spot < REACH, turn(left, -(8 * t + 8 - REACH)), turn(right, PAIR - REACH - 8 * t)
                )
                for g in range(groups):
                    plane = ref[1 + tiles * g + t, here]
                    mine = group == g
                    value = jnp.where(
                        mine & (spot >= REACH) & (spot < STRIP), turn(plane, PAIR * g + REACH), value
                    )
                    value = jnp.where(
                        mine & (spot >= STRIP) & (spot < PAIR - REACH),
                        turn(plane, PAIR * g + PAIR - REACH), value,
                    )
                ref[first_tile + t, here] = value
            return 0

        lax.fori_loop(0, heat_chunks, fill, 0)

    def close_ring(ref, index, count):
        last = at(count)
        ref[(*index, slice(7, 8))] = ref[(*index, slice(last - 1, last))]
        ref[(*index, slice(last, last + 1))] = ref[(*index, slice(8, 9))]

    def wrap(ref, index):
        low = ref[(*index, high_wrap - 1)]
        high = ref[(*index, first_tile)]
        wide = lax.broadcasted_iota(jnp.int32, low.shape, 1)
        ref[(*index, low_wrap)] = jnp.where(wide >= PAIR, turn(low, PAIR), 0.0)
        ref[(*index, high_wrap)] = jnp.where(wide < cols - PAIR, turn(high, -PAIR), 0.0)

    def over(planes, body, unroll):
        lax.fori_loop(planes[0], planes[-1] + 1, lambda p, _: (body(p), 0)[1], 0, unroll=unroll)

    materials = traits.shape[1]
    spots = power_table.shape[0]

    def put(ref, index, chunk, count, value):
        ref[(*index, slice(at(chunk), at(chunk) + 8))] = value
        if chunk == 0:
            ref[(*index, slice(at(count), at(count) + 1))] = value[0:1]
        if chunk == count - 1:
            ref[(*index, slice(7, 8))] = value[7:8]

    def to_ring(ref, p, values):
        found = list(values)
        if len(found) > chunks:
            found = found[:own_chunks] + [jnp.where(row8 < EDGE, found[-2], found[-1])]
        for chunk, value in enumerate(found):
            put(ref, (p,), chunk, chunks, value)

    def prepare(p):
        kept = []
        for chunk in range(heat_chunks):
            here = slice(at(chunk), at(chunk) + 8)
            ids, patches = lab[p, here], pat[p, here]
            inside = ids >= 0
            bits = bits_of(ids, materials)
            found = [pick(bits, [traits[q, m] for m in range(materials)], materials) for q in range(4)]
            put(cond, (p,), chunk, heat_chunks, jnp.where(inside, found[0], 0.0))
            rate_s[p, here] = jnp.where(inside, TIME_STEP / found[1], 0.0)
            tile_bits = bits_of(patches, spots)
            pow_s[p, here] = pick(tile_bits, [power_table[t] for t in range(spots)], spots)
            kept.append((
                jnp.where(inside, found[2] * quarter_inverse, 0.0),
                jnp.where(inside, found[3], 0.0), jnp.where(inside, 1.0, 0.0),
            ))
        for ref, values in zip((mod, strain, mask), zip(*kept)):
            to_ring(ref, p, values)
        close_ring(temp, (p,), heat_chunks)

    over(main, prepare, 2)
    over(strips, prepare, 2)
    for ref in (cond, temp, mod):
        wrap(ref, ())

    def conduct(a, b):
        return 2.0 * a * b / jnp.maximum(a + b, 0.25)

    def conductance(p):
        for chunk in range(heat_chunks):
            here = slice(at(chunk), at(chunk) + 8)
            mine = cond[p, here]
            put(gx_s, (p,), chunk, heat_chunks, conduct(mine, cond[p, at(chunk) + 1 : at(chunk) + 9]))
            gy_s[p, here] = conduct(mine, turn(mine, -1))
            gz_s[p, here] = conduct(mine, cond[p + 1, here])

    over(main, conductance, 4)
    over(range(low_wrap, high_wrap), conductance, 5)

    def heat(p, chunk, source):
        start = at(chunk)
        here = slice(start, start + 8)
        before, after = slice(start - 1, start + 7), slice(start + 1, start + 9)
        centre = source[p, here]
        flux = gx_s[p, here] * (source[p, after] - centre) - gx_s[p, before] * (centre - source[p, before])
        flow_y = gy_s[p, here] * (turn(centre, -1) - centre)
        flux = flux + (flow_y - turn(flow_y, 1))
        flux = flux + gz_s[p, here] * (source[p + 1, here] - centre)
        flux = flux - gz_s[p - 1, here] * (centre - source[p - 1, here])
        return centre + rate_s[p, here] * (flux + pow_s[p, here])

    def first_step(p):
        for chunk in range(heat_chunks):
            put(temp2, (p,), chunk, heat_chunks, heat(p, chunk, temp))

    over(main, first_step, 4)
    over(strips, first_step, 4)
    wrap(temp2, ())

    def patched(value, edge, g):
        left = turn(edge, -(PAIR * g + REACH))
        right = turn(edge, -(PAIR * g + PAIR - REACH))
        return jnp.where(lane < EDGE, left, jnp.where(lane >= cols - EDGE, right, value))

    def strain_of(p, values):
        if len(values) > chunks:
            values = values[:own_chunks] + [jnp.where(row8 < EDGE, values[-2], values[-1])]
        for chunk, value in enumerate(values):
            here = slice(at(chunk), at(chunk) + 8)
            value = strain[p, here] * value
            put(strain, (p,), chunk, chunks, value)
            put(both, (p,), chunk, chunks, mod[p, here] * value)

    def second_strip(p):
        values = [heat(p, chunk, temp2) for chunk in range(heat_chunks)]
        for chunk, value in enumerate(values):
            temp[p, at(chunk) : at(chunk) + 8] = value
        strain_of(p, values)

    over(strips, second_strip, 4)
    for g in range(groups):
        def second_main(t, g=g):
            p = 1 + tiles * g + t
            values = []
            for chunk in range(heat_chunks):
                edge = temp[first_tile + t, at(chunk) : at(chunk) + 8]
                values.append(patched(heat(p, chunk, temp2), edge, g))
            for chunk in range(own_chunks):
                warmed[p - 1, 8 * chunk : 8 * chunk + 8] = values[chunk]
            strain_of(p, values)

        over(range(tiles), second_main, 4)
    results = [pltpu.make_async_copy(warmed, warmed_out, out_sem.at[0])]
    results[0].start()
    for ref in (strain, both):
        wrap(ref, ())

    def mended(ref, index, z, t, g, chunk):
        here = slice(at(chunk), at(chunk) + 8)
        return patched(ref[(*index, 1 + z, here)], ref[(*index, first_tile + t, here)], g)

    def mend(body, carry):
        for g in range(groups):
            def step(t, carry, g=g):
                for chunk in range(own_chunks):
                    carry = body(tiles * g + t, t, g, chunk, carry)
                return carry

            carry = lax.fori_loop(0, tiles, step, carry, unroll=tiles)
        return carry

    def sweep(chunk_list, parts, emit, unroll):
        for chunk in chunk_list:
            stream_closed(
                1, layers, lambda p, chunk=chunk: parts(p, at(chunk)),
                lambda p, out, chunk=chunk: emit(p, chunk, out), unroll,
            )
            stream_open(
                first_tile, tiles, lambda p, chunk=chunk: parts(p, at(chunk)),
                lambda p, out, chunk=chunk: emit(p, chunk, out),
            )

    def matrix_emit(p, chunk, out):
        here = slice(at(chunk), at(chunk) + 8)
        diagonal = (4.0 * (ANCHOR + K_TOTAL)) * mod[p, here] - 1.0
        for c, value in enumerate(matrix_finish(out)):
            mats[c, p, 8 * chunk : 8 * chunk + 8] = value + diagonal if c < 3 else value

    sweep(range(chunks), lambda p, where: matrix_parts(three(mod, (p,), where)), matrix_emit, layers - 1)

    def load_parts(p, where):
        return tuple(a for ref in (strain, mod, both) for a in gradient_parts(three(ref, (p,), where)))

    def keep_basis(k, p, chunk, c, value):
        here = slice(at(chunk), at(chunk) + 8)
        put(v[k], (c, p), chunk, chunks, value)
        put(v[k], (3 + c, p), chunk, chunks, mod[p, here] * value)

    def load_emit(p, chunk, out):
        here = slice(at(chunk), at(chunk) + 8)
        m, s, inside = mod[p, here], strain[p, here], mask[p, here]
        found = [gradient_finish(out[5 * i : 5 * i + 5]) for i in range(3)]
        for c in range(3):
            value = -inside * (m * found[0][c] + s * found[1][c] + found[2][c])
            keep_basis(0, p, chunk, c, value)

    sweep(range(chunks), load_parts, load_emit, layers - 1)

    def settle(k, more):
        if more:
            for c in range(6):
                wrap(v[k], (c,))

        def body(z, t, g, chunk, carry):
            odd, even = carry
            rows_here = slice(8 * chunk, 8 * chunk + 8)
            for c in range(3):
                value = mended(v[k], (c,), z, t, g, chunk)
                vown[k, c, z, rows_here] = value
                even = even + value * value
                if odd is not None:
                    odd = odd + value * vown[k - 1, c, z, rows_here]
            return odd, even

        return body

    def shares(k):
        found = []
        for step in range(1, nz):
            there = lax.rem(iz + step, nz)
            found.append(
                pltpu.make_async_remote_copy(
                    src_ref=vown.at[k, :, pl.ds(there * share, share)],
                    dst_ref=vrecv.at[k, step - 1],
                    send_sem=vsend_sem.at[k, step - 1], recv_sem=vrecv_sem.at[k, step - 1],
                    device_id=(ix, iy, there), device_id_type=MESH,
                )
            )
        return found

    def share_basis(k):
        for copy in shares(k):
            copy.start()

    moment_s[0] = mend(settle(0, True), (None, empty))[1]
    share_basis(0)

    def apply(k, chunk_list):
        def parts(p, where):
            return operator_parts(*[three(v[k], (c, p), where) for c in range(3)]) + operator_parts(
                *[three(v[k], (3 + c, p), where) for c in range(3)]
            )

        def emit(p, chunk, out):
            here = slice(at(chunk), at(chunk) + 8)
            m, inside = mod[p, here], mask[p, here]
            u = [v[k][c, p, here] for c in range(3)]
            zz, xx, yy, zx, zy, xy = [mats[c, p, 8 * chunk : 8 * chunk + 8] for c in range(6)]
            grown = (
                zz * u[0] + zx * u[1] + zy * u[2],
                zx * u[0] + xx * u[1] + xy * u[2],
                zy * u[0] + xy * u[1] + yy * u[2],
            )
            first, second = operator_finish(out[:9]), operator_finish(out[9:])
            for c in range(3):
                value = grown[c] - m * first[c] - second[c]
                if len(chunk_list) > own_chunks:
                    keep_basis(k + 1, p, chunk, c, inside * value)
                else:
                    v[k + 1][c, p, here] = value

        sweep(chunk_list, parts, emit, layers - 1)

    def grow(k, _):
        apply(k, range(chunks))
        odd, even = mend(settle(k + 1, True), (empty, empty))
        moment_s[2 * k + 1] = odd
        moment_s[2 * k + 2] = even
        share_basis(k + 1)
        return 0

    for k in range(ITERS - 1):
        grow(k, 0)
    apply(ITERS - 1, range(own_chunks))
    odd, even = mend(settle(ITERS, False), (empty, empty))
    moment_s[2 * ITERS - 1] = odd
    moment_s[2 * ITERS] = even

    lane8 = lax.broadcasted_iota(jnp.int32, (1, cols), 1)
    row = jnp.zeros((1, cols), jnp.float32)
    for k in range(2 * ITERS):
        line = jnp.sum(moment_s[k], axis=0, keepdims=True)
        row = jnp.where(lane8 == k, jnp.sum(line, axis=1, keepdims=True), row)
    red_src[...] = row
    red_buf[me] = row

    def spread(k):
        there = lax.rem(me + k, total)
        return pltpu.make_async_remote_copy(
            src_ref=red_src, dst_ref=red_buf.at[me], send_sem=rsend_sem.at[k],
            recv_sem=rrecv_sem.at[k], device_id=coords(there), device_id_type=MESH,
        )

    def collect(k):
        there = lax.rem(me + total - k, total)
        return pltpu.make_async_remote_copy(
            src_ref=red_src, dst_ref=red_buf.at[there], send_sem=rsend_sem.at[k],
            recv_sem=rrecv_sem.at[k], device_id=coords(there), device_id_type=MESH,
        )

    def start(k, _):
        spread(k).start()
        return 0

    def finish(k, _):
        collect(k).wait_recv()
        return 0

    def sent(k, _):
        spread(k).wait_send()
        return 0

    lax.fori_loop(1, total, start, 0, unroll=4)
    share_basis(ITERS)
    lax.fori_loop(1, total, finish, 0, unroll=4)

    def add(k, acc):
        return acc + red_buf[k]

    summed = lax.fori_loop(0, total, add, jnp.zeros((1, cols), jnp.float32), unroll=4)
    m = [
        jnp.sum(jnp.where(lane8 == k, summed, 0.0), axis=1, keepdims=True) for k in range(2 * ITERS)
    ]

    def inner(a, b):
        value = None
        for i, x in enumerate(a):
            for j, y in enumerate(b):
                if x is not None and y is not None:
                    term = x * y * m[i + j]
                    value = term if value is None else value + term
        return value

    def plus(a, factor, b):
        out = []
        for x, y in zip(a, b):
            if y is None:
                out.append(x)
            else:
                out.append(factor * y if x is None else x + factor * y)
        return out

    one = jnp.ones((1, 1), jnp.float32)
    size = ITERS + 1
    res = [one] + [None] * ITERS
    dire = list(res)
    sol = [None] * size
    rr = m[0]
    for number in range(ITERS):
        image = plus(list(dire), 1.0, [None] + dire[:-1])
        alpha = rr / inner(dire, image)
        sol = plus(sol, alpha, dire)
        res = plus(res, -alpha, image)
        if number + 1 < ITERS:
            new = inner(res, res)
            dire = plus(res, new / rr, dire)
            rr = new
    res = [shift_scalar * x for x in res]

    for step in range(nz):
        where = pl.ds(pl.multiple_of(lax.rem(iz + nz - step, nz) * cols, cols), cols)
        for index, (weights, held, target) in enumerate(
            ((sol[:ITERS], solution, solution_out), (res, residual, residual_out))
        ):
            if step:
                for k in range(ITERS) if index == 0 else (ITERS,):
                    shares(k)[step - 1].wait_recv()

            def combine(z, _, step=step, weights=weights, held=held):
                for c in range(3):
                    value = None
                    for k, weight in enumerate(weights):
                        part = vown[k, c, iz * share + z] if step == 0 else vrecv[k, step - 1, c, z]
                        value = weight * part if value is None else value + weight * part
                    held[step, c, z] = value
                return 0

            lax.fori_loop(0, share, combine, 0, unroll=4)
            results.append(
                pltpu.make_async_copy(
                    held.at[step], target.at[:, :, :, where], out_sem.at[1 + 2 * step + index]
                )
            )
            results[-1].start()

    for target, _, copies, _ in moves:
        @pl.when(target)
        def _(copies=copies):
            for copy in copies:
                copy.wait_send()
    for k in range(ITERS + 1):
        for copy in shares(k):
            copy.wait_send()
    lax.fori_loop(1, total, sent, 0)
    for copy in results:
        copy.wait()


def per_device(sizes, *arrays):
    nx, ny, nz = sizes
    layers, rows, cols = arrays[0].shape
    total = nx * ny * nz
    share = layers // nz
    f32, i32 = jnp.float32, jnp.int32
    vmem = pltpu.VMEM
    dma = pltpu.SemaphoreType.DMA
    out = jax.ShapeDtypeStruct((3, share, rows, cols * nz), f32)
    ring = rows + (8 if nx <= 2 else 16)
    planes = layers + 4 + layers * PAIR // cols
    heated = (planes, ring + 16, cols)
    kept = (planes, rows + 24, cols)
    half = vmem((nz, 3, share, rows, cols), f32)
    return pl.pallas_call(
        functools.partial(kernel, sizes),
        out_shape=(jax.ShapeDtypeStruct((layers, rows, cols), f32), out, out),
        in_specs=[pl.BlockSpec(memory_space=pltpu.HBM)] * 5,
        out_specs=[pl.BlockSpec(memory_space=pl.ANY)] * 3,
        scratch_shapes=[
            pltpu.SMEM(arrays[3].shape, f32), pltpu.SMEM(arrays[4].shape, f32), dma((2,)),
            vmem((layers, rows, cols), f32), half, half,
            vmem((ITERS + 1, 3, layers, rows, cols), f32),
            vmem((2 * ITERS + 1, 8, cols), f32), dma((1 + 2 * nz,)),
            vmem(heated, f32), vmem(heated, f32), vmem(heated, i32), vmem(heated, i32),
            *[vmem(heated, f32)] * 6,
            *[vmem(kept, f32)] * 4,
            vmem((6, planes, rows + 8, cols), f32),
            *[vmem((6, *kept), f32)] * ITERS, vmem((3, *kept), f32),
            vmem((ITERS + 1, nz - 1, 3, share, rows, cols), f32),
            vmem((2, rows, cols), f32), vmem((2, 2, rows, cols), i32),
            vmem((2, ring, cols), f32), vmem((2, 2, ring, cols), i32),
            vmem((1, cols), f32), vmem((total, 1, cols), f32),
            dma((3,)), dma((8, 3)), dma((8, 3)),
            dma((ITERS + 1, nz - 1)), dma((ITERS + 1, nz - 1)), dma((total,)), dma((total,)),
        ],
        compiler_params=pltpu.CompilerParams(
            collective_id=0, has_side_effects=True, vmem_limit_bytes=52 * 1024 * 1024
        ),
    )(*[pltpu.with_memory_space_constraint(a, pltpu.HBM) for a in arrays])


def solution(mesh):
    sizes = tuple(mesh.shape[axis] for axis in ("gx", "gy", "gz"))
    split = P(None, "gx", ("gy", "gz"))
    out = P(None, "gz", "gx", "gy")
    return jax.shard_map(
        functools.partial(per_device, sizes),
        mesh=mesh,
        in_specs=(split, split, split, P(), P()),
        out_specs=(split, out, out),
        check_vma=False,
    )
```

time: 44.5 us -> 40.9 us (0.919)
  Pallas kernels: 41.6 us -> 37.9 us
    pallas_call x1, Pallas kernels: 41.6 us -> 37.9 us  [per_device(): pl.pallas_call(functools.partial(kernel, sizes), out_shape=(jax.ShapeDtyp...]
where the time goes in v1:
time: 40.9 us; the launch traced here: 40.7 us
  Pallas kernels  37.9 us (93%)
  local copies, waits for them, and re-layouts  2.15 us (5%)
  between operations  0.64 us (2%)
    pallas_call x1, Pallas kernels, per_device(): pl.pallas_call(functools.partial(kernel, sizes), out_shape=(jax.ShapeDtyp...  37.9 us
    unnamed x3, local copies, waits for them, and re-layouts  2.15 us

profile of v1, /device:TPU:0, one launch (start us, length us, event | category | flops | bytes accessed | tf_op | source)
XLA Modules:
  0.0 40.7 jit_solution(15989178247739487344)
XLA Ops:
  0.6 37.9 %shard_map.76 = (f32[16,16,128]{2,1,0:T(8,128)S(1)}, f32[3,8,16,256]{3,2,1,0:T(8,128)S(1)}, f32[3,8,16,256]{3,2,1,0:T(8,128)S(1)}) custom-call(f32[16,16,128]{2,1,0:T(8,128)} %kelvin.1, s32[16,16,128]{2,1,0:T(8,128)} %label.1, s32[16,16,128]{2,1,0:T(8,128)} %patch.1, f32[4,4]{1,0:T(4,128)} %traits_in.1, f32[16]{0:T(128)} %power_in.1), custom_call_target="tpu_custom_call" | custom-call | tf_op jit(solution)/shard_map/pallas_call | solution.py:745
  38.6 0.7 %copy.11 = f32[16,16,128]{2,1,0:T(8,128)} copy(f32[16,16,128]{2,1,0:T(8,128)S(1)} %get-tuple-element.6) | data formatting | bytes 262144
  39.2 0.7 %copy.12 = f32[3,8,16,256]{3,2,1,0:T(8,128)} copy(f32[3,8,16,256]{3,2,1,0:T(8,128)S(1)} %get-tuple-element.7) | data formatting | bytes 786432
  40.0 0.7 %copy.13 = f32[3,8,16,256]{3,2,1,0:T(8,128)} copy(f32[3,8,16,256]{3,2,1,0:T(8,128)S(1)} %get-tuple-element.8) | data formatting | bytes 786432

commit v2 on v1

--- a/solution.py
+++ b/solution.py
@@ -11,6 +11,7 @@
 HALO = 8
 REACH = 6
 EDGE = 4
+EARLY = 4
 STRIP = 16
 PAIR = 2 * STRIP
 TIME_STEP = 0.03
@@ -165,18 +166,19 @@
 def kernel(
     sizes,
     kelvin, label, patch, traits_in, power_in,
-    warmed_out, solution_out, residual_out,
-    traits, power_table, table_sem, warmed, solution, residual, vown, moment_s, out_sem,
+    warmed, solution, residual,
+    traits, power_table, table_sem, vown, moment_s,
     temp, temp2, lab, pat, cond, rate_s, pow_s, gx_s, gy_s, gz_s,
     mod, strain, both, mask, mats, v0, v1, v2, v3,
-    vrecv, pack_f, pack_i, got_f, got_i, red_src, red_buf,
-    local_sem, send_sem, recv_sem, vsend_sem, vrecv_sem, rsend_sem, rrecv_sem,
+    vrecv, late_src, late_got, pack_f, pack_i, got_f, got_i, red_src, red_buf,
+    local_sem, send_sem, recv_sem, vsend_sem, vrecv_sem, late_send, late_recv, rsend_sem, rrecv_sem,
 ):
     nx, ny, nz = sizes
     v = (v0, v1, v2, v3)
     nc, total = ny * nz, nx * ny * nz
     layers, rows, cols = kelvin.shape
     share = layers // nz
+    early = share * EARLY // 8
     own_chunks = rows // 8
     chunks = own_chunks + 1
     heat_chunks = own_chunks + (1 if nx <= 2 else 2)
@@ -270,16 +272,6 @@
     moves = [transfers(i) for i in range(len(DIRECTIONS))]
     for copy in local:
         copy.wait()
-    pl.semaphore_wait(barrier, total - 1)
-    for target, _, copies, dc in moves:
-        if dc != 0:
-            continue
-
-        @pl.when(target)
-        def _(copies=copies):
-            for copy in copies:
-                copy.start()
-
     wide_lane = lax.broadcasted_iota(jnp.int32, (rows, cols), 1) // HALO
     for side in (0, 1):
         for index, ref in enumerate(raw):
@@ -292,14 +284,16 @@
             else:
                 pack_i[side, index - 1] = packed
 
-    for target, _, copies, dc in moves:
-        if dc == 0:
-            continue
-
-        @pl.when(target)
-        def _(copies=copies):
-            for copy in copies:
-                copy.start()
+    pl.semaphore_wait(barrier, total - 1)
+    for wanted in (True, False):
+        for target, _, copies, dc in moves:
+            if (dc == 0) != wanted:
+                continue
+
+            @pl.when(target)
+            def _(copies=copies):
+                for copy in copies:
+                    copy.start()
 
     lane = lax.broadcasted_iota(jnp.int32, (8, cols), 1)
     row8 = lax.broadcasted_iota(jnp.int32, (8, cols), 0)
@@ -314,39 +308,33 @@
     shift_scalar = 3.0 * (traits[2, 0] + traits[2, 1] + traits[2, 2] + traits[2, 3])
     quarter_inverse = 0.25 / jnp.full((8, cols), shift_scalar, jnp.float32)
 
-    for _, origin, copies, _ in moves:
-        @pl.when(origin)
-        def _(copies=copies):
-            for copy in copies:
-                copy.wait_recv()
-
     group, spot = lane // PAIR, lane % PAIR
-    for index, ref in enumerate(raw):
-        def fill(chunk, _, index=index, ref=ref):
-            pos = pl.multiple_of(8 * chunk, 8)
-            here = pl.ds(pl.multiple_of(8 * chunk + 8, 8), 8)
+    from_left, from_right = spot < REACH, spot >= PAIR - REACH
+    own_left = [(group == g) & (spot >= REACH) & (spot < STRIP) for g in range(groups)]
+    own_right = [(group == g) & (spot >= STRIP) & (spot < PAIR - REACH) for g in range(groups)]
+
+    def inner_strip(chunk):
+        here = slice(at(chunk), at(chunk) + 8)
+        for ref in raw:
+            for t in range(tiles):
+                value = jnp.zeros((8, cols), ref.dtype)
+                for g in range(groups):
+                    plane = ref[1 + tiles * g + t, here]
+                    value = jnp.where(own_left[g], turn(plane, PAIR * g + REACH), value)
+                    value = jnp.where(own_right[g], turn(plane, PAIR * g + PAIR - REACH), value)
+                ref[first_tile + t, here] = value
+
+    def outer_strip(chunk):
+        here, pos = slice(at(chunk), at(chunk) + 8), slice(8 * chunk, 8 * chunk + 8)
+        for index, ref in enumerate(raw):
             left, right = (
-                got_f[side, pl.ds(pos, 8)] if index == 0 else got_i[side, index - 1, pl.ds(pos, 8)]
-                for side in (1, 0)
+                got_f[side, pos] if index == 0 else got_i[side, index - 1, pos] for side in (1, 0)
             )
             for t in range(tiles):
-                value = jnp.where(
-                    spot < REACH, turn(left, -(8 * t + 8 - REACH)), turn(right, PAIR - REACH - 8 * t)
-                )
-                for g in range(groups):
-                    plane = ref[1 + tiles * g + t, here]
-                    mine = group == g
-                    value = jnp.where(
-                        mine & (spot >= REACH) & (spot < STRIP), turn(plane, PAIR * g + REACH), value
-                    )
-                    value = jnp.where(
-                        mine & (spot >= STRIP) & (spot < PAIR - REACH),
-                        turn(plane, PAIR * g + PAIR - REACH), value,
-                    )
+                value = ref[first_tile + t, here]
+                value = jnp.where(from_left, turn(left, -(8 * t + 8 - REACH)), value)
+                value = jnp.where(from_right, turn(right, PAIR - REACH - 8 * t), value)
                 ref[first_tile + t, here] = value
-            return 0
-
-        lax.fori_loop(0, heat_chunks, fill, 0)
 
     def close_ring(ref, index, count):
         last = at(count)
@@ -373,16 +361,16 @@
         if chunk == count - 1:
             ref[(*index, slice(7, 8))] = value[7:8]
 
-    def to_ring(ref, p, values):
+    def to_ring(ref, p, first, values):
         found = list(values)
-        if len(found) > chunks:
-            found = found[:own_chunks] + [jnp.where(row8 < EDGE, found[-2], found[-1])]
-        for chunk, value in enumerate(found):
-            put(ref, (p,), chunk, chunks, value)
-
-    def prepare(p):
+        if first + len(found) > chunks:
+            found = found[:-2] + [jnp.where(row8 < EDGE, found[-2], found[-1])]
+        for i, value in enumerate(found):
+            put(ref, (p,), first + i, chunks, value)
+
+    def prepare(p, chunk_list):
         kept = []
-        for chunk in range(heat_chunks):
+        for chunk in chunk_list:
             here = slice(at(chunk), at(chunk) + 8)
             ids, patches = lab[p, here], pat[p, here]
             inside = ids >= 0
@@ -397,11 +385,27 @@
                 jnp.where(inside, found[3], 0.0), jnp.where(inside, 1.0, 0.0),
             ))
         for ref, values in zip((mod, strain, mask), zip(*kept)):
-            to_ring(ref, p, values)
+            to_ring(ref, p, chunk_list[0], values)
+
+    own_list, halo_list = range(own_chunks), range(own_chunks, heat_chunks)
+    over(main, lambda p: prepare(p, own_list), 4)
+    for chunk in own_list:
+        inner_strip(chunk)
+    for _, origin, copies, _ in moves:
+        @pl.when(origin)
+        def _(copies=copies):
+            for copy in copies:
+                copy.wait_recv()
+
+    for chunk in own_list:
+        outer_strip(chunk)
+    for chunk in halo_list:
+        inner_strip(chunk)
+        outer_strip(chunk)
+    over(main, lambda p: prepare(p, halo_list), 4)
+    over(strips, lambda p: prepare(p, range(heat_chunks)), tiles)
+    for p in (*main, *strips):
         close_ring(temp, (p,), heat_chunks)
-
-    over(main, prepare, 2)
-    over(strips, prepare, 2)
     for ref in (cond, temp, mod):
         wrap(ref, ())
 
@@ -416,8 +420,8 @@
             gy_s[p, here] = conduct(mine, turn(mine, -1))
             gz_s[p, here] = conduct(mine, cond[p + 1, here])
 
-    over(main, conductance, 4)
-    over(range(low_wrap, high_wrap), conductance, 5)
+    for p in (*main, *range(low_wrap, high_wrap)):
+        conductance(p)
 
     def heat(p, chunk, source):
         start = at(chunk)
@@ -435,8 +439,8 @@
         for chunk in range(heat_chunks):
             put(temp2, (p,), chunk, heat_chunks, heat(p, chunk, temp))
 
-    over(main, first_step, 4)
-    over(strips, first_step, 4)
+    for p in (*strips, *main):
+        first_step(p)
     wrap(temp2, ())
 
     def patched(value, edge, g):
@@ -459,7 +463,8 @@
             temp[p, at(chunk) : at(chunk) + 8] = value
         strain_of(p, values)
 
-    over(strips, second_strip, 4)
+    for p in strips:
+        second_strip(p)
     for g in range(groups):
         def second_main(t, g=g):
             p = 1 + tiles * g + t
@@ -471,9 +476,8 @@
                 warmed[p - 1, 8 * chunk : 8 * chunk + 8] = values[chunk]
             strain_of(p, values)
 
-        over(range(tiles), second_main, 4)
-    results = [pltpu.make_async_copy(warmed, warmed_out, out_sem.at[0])]
-    results[0].start()
+        for t in range(tiles):
+            second_main(t)
     for ref in (strain, both):
         wrap(ref, ())
 
@@ -552,7 +556,7 @@
             there = lax.rem(iz + step, nz)
             found.append(
                 pltpu.make_async_remote_copy(
-                    src_ref=vown.at[k, :, pl.ds(there * share, share)],
+                    src_ref=vown.at[k, :, pl.ds(there * share, early)],
                     dst_ref=vrecv.at[k, step - 1],
                     send_sem=vsend_sem.at[k, step - 1], recv_sem=vrecv_sem.at[k, step - 1],
                     device_id=(ix, iy, there), device_id_type=MESH,
@@ -689,31 +693,80 @@
             rr = new
     res = [shift_scalar * x for x in res]
 
-    for step in range(nz):
-        where = pl.ds(pl.multiple_of(lax.rem(iz + nz - step, nz) * cols, cols), cols)
-        for index, (weights, held, target) in enumerate(
-            ((sol[:ITERS], solution, solution_out), (res, residual, residual_out))
-        ):
-            if step:
-                for k in range(ITERS) if index == 0 else (ITERS,):
-                    shares(k)[step - 1].wait_recv()
-
-            def combine(z, _, step=step, weights=weights, held=held):
+    sol = [None if x is None else jnp.broadcast_to(x, (8, cols)) for x in sol[:ITERS]]
+    res = [jnp.broadcast_to(x, (8, cols)) for x in res]
+
+    def blend(weights, part):
+        value = None
+        for k, weight in enumerate(weights):
+            value = weight * part(k) if value is None else value + weight * part(k)
+        return value
+
+    row_tiles = [slice(8 * chunk, 8 * chunk + 8) for chunk in range(own_chunks)]
+
+    def lates():
+        found = []
+        for step in range(1, nz):
+            there = lax.rem(iz + step, nz)
+            for part in (0, 1):
+                found.append(
+                    pltpu.make_async_remote_copy(
+                        src_ref=late_src.at[step - 1, part], dst_ref=late_got.at[step - 1, part],
+                        send_sem=late_send.at[step - 1, part], recv_sem=late_recv.at[step - 1, part],
+                        device_id=(ix, iy, there), device_id_type=MESH,
+                    )
+                )
+        return found
+
+    late_copies = lates()
+    for step in range(1, nz):
+        base = lax.rem(iz + step, nz) * share + early
+        for part, weights in enumerate((sol, res)):
+            def finish_late(z, _, step=step, part=part, weights=weights, base=base):
                 for c in range(3):
-                    value = None
-                    for k, weight in enumerate(weights):
-                        part = vown[k, c, iz * share + z] if step == 0 else vrecv[k, step - 1, c, z]
-                        value = weight * part if value is None else value + weight * part
-                    held[step, c, z] = value
+                    for here in row_tiles:
+                        late_src[step - 1, part, c, z, here] = blend(
+                            weights, lambda k: vown[k, c, base + z, here]
+                        )
                 return 0
 
-            lax.fori_loop(0, share, combine, 0, unroll=4)
-            results.append(
-                pltpu.make_async_copy(
-                    held.at[step], target.at[:, :, :, where], out_sem.at[1 + 2 * step + index]
-                )
-            )
-            results[-1].start()
+            lax.fori_loop(0, share - early, finish_late, 0, unroll=True)
+            late_copies[2 * (step - 1) + part].start()
+
+    def lanes_of(step):
+        return pl.ds(pl.multiple_of(lax.rem(iz + nz - step, nz) * cols, cols), cols)
+
+    for part, (weights, target) in enumerate(((sol, solution), (res, residual))):
+        def finish_own(z, _, weights=weights, target=target):
+            for c in range(3):
+                for here in row_tiles:
+                    target[c, z, here, lanes_of(0)] = blend(
+                        weights, lambda k: vown[k, c, iz * share + z, here]
+                    )
+            return 0
+
+        lax.fori_loop(0, share, finish_own, 0, unroll=4)
+    for step in range(1, nz):
+        for part, (weights, target) in enumerate(((sol, solution), (res, residual))):
+            for k in range(ITERS) if part == 0 else (ITERS,):
+                shares(k)[step - 1].wait_recv()
+
+            def finish_early(z, _, step=step, weights=weights, target=target):
+                for c in range(3):
+                    for here in row_tiles:
+                        target[c, z, here, lanes_of(step)] = blend(
+                            weights, lambda k: vrecv[k, step - 1, c, z, here]
+                        )
+                return 0
+
+            lax.fori_loop(0, early, finish_early, 0, unroll=True)
+    for step in range(1, nz):
+        for part, target in enumerate((solution, residual)):
+            late_copies[2 * (step - 1) + part].wait_recv()
+            for z in range(share - early):
+                for c in range(3):
+                    for here in row_tiles:
+                        target[c, early + z, here, lanes_of(step)] = late_got[step - 1, part, c, z, here]
 
     for target, _, copies, _ in moves:
         @pl.when(target)
@@ -723,9 +776,9 @@
     for k in range(ITERS + 1):
         for copy in shares(k):
             copy.wait_send()
-    lax.fori_loop(1, total, sent, 0)
-    for copy in results:
-        copy.wait()
+    for copy in late_copies:
+        copy.wait_send()
+    lax.fori_loop(1, total, sent, 0, unroll=4)
 
 
 def per_device(sizes, *arrays):
@@ -733,39 +786,42 @@
     layers, rows, cols = arrays[0].shape
     total = nx * ny * nz
     share = layers // nz
+    early = share * EARLY // 8
     f32, i32 = jnp.float32, jnp.int32
     vmem = pltpu.VMEM
     dma = pltpu.SemaphoreType.DMA
     out = jax.ShapeDtypeStruct((3, share, rows, cols * nz), f32)
+    shapes = (jax.ShapeDtypeStruct((layers, rows, cols), f32), out, out)
     ring = rows + (8 if nx <= 2 else 16)
     planes = layers + 4 + layers * PAIR // cols
     heated = (planes, ring + 16, cols)
     kept = (planes, rows + 24, cols)
-    half = vmem((nz, 3, share, rows, cols), f32)
+    late = (nz - 1, 2, 3, share - early, rows, cols)
     return pl.pallas_call(
         functools.partial(kernel, sizes),
-        out_shape=(jax.ShapeDtypeStruct((layers, rows, cols), f32), out, out),
+        out_shape=shapes,
         in_specs=[pl.BlockSpec(memory_space=pltpu.HBM)] * 5,
-        out_specs=[pl.BlockSpec(memory_space=pl.ANY)] * 3,
+        out_specs=[pl.BlockSpec(memory_space=pltpu.VMEM)] * 3,
         scratch_shapes=[
             pltpu.SMEM(arrays[3].shape, f32), pltpu.SMEM(arrays[4].shape, f32), dma((2,)),
-            vmem((layers, rows, cols), f32), half, half,
             vmem((ITERS + 1, 3, layers, rows, cols), f32),
-            vmem((2 * ITERS + 1, 8, cols), f32), dma((1 + 2 * nz,)),
+            vmem((2 * ITERS + 1, 8, cols), f32),
             vmem(heated, f32), vmem(heated, f32), vmem(heated, i32), vmem(heated, i32),
             *[vmem(heated, f32)] * 6,
             *[vmem(kept, f32)] * 4,
             vmem((6, planes, rows + 8, cols), f32),
             *[vmem((6, *kept), f32)] * ITERS, vmem((3, *kept), f32),
-            vmem((ITERS + 1, nz - 1, 3, share, rows, cols), f32),
+            vmem((ITERS + 1, nz - 1, 3, early, rows, cols), f32),
+            vmem(late, f32), vmem(late, f32),
             vmem((2, rows, cols), f32), vmem((2, 2, rows, cols), i32),
             vmem((2, ring, cols), f32), vmem((2, 2, ring, cols), i32),
             vmem((1, cols), f32), vmem((total, 1, cols), f32),
             dma((3,)), dma((8, 3)), dma((8, 3)),
-            dma((ITERS + 1, nz - 1)), dma((ITERS + 1, nz - 1)), dma((total,)), dma((total,)),
+            dma((ITERS + 1, nz - 1)), dma((ITERS + 1, nz - 1)),
+            dma((nz - 1, 2)), dma((nz - 1, 2)), dma((total,)), dma((total,)),
         ],
         compiler_params=pltpu.CompilerParams(
-            collective_id=0, has_side_effects=True, vmem_limit_bytes=52 * 1024 * 1024
+            collective_id=0, has_side_effects=True, vmem_limit_bytes=48 * 1024 * 1024
         ),
     )(*[pltpu.with_memory_space_constraint(a, pltpu.HBM) for a in arrays])
 

time: 40.9 us -> 35.5 us (0.87)
  Pallas kernels: 37.9 us -> 32.6 us
    pallas_call x1, Pallas kernels: 37.9 us -> 32.6 us  [per_device(): pl.pallas_call(functools.partial(kernel, sizes), out_shape=shapes, in_spe...]
where the time goes in v2:
time: 35.5 us; the launch traced here: 35.4 us
  Pallas kernels  32.6 us (92%)
  local copies, waits for them, and re-layouts  2.15 us (6%)
  between operations  0.64 us (2%)
    pallas_call x1, Pallas kernels, per_device(): pl.pallas_call(functools.partial(kernel, sizes), out_shape=shapes, in_spe...  32.6 us
    unnamed x3, local copies, waits for them, and re-layouts  2.15 us

profile of v2, /device:TPU:0, one launch (start us, length us, event | category | flops | bytes accessed | tf_op | source)
XLA Modules:
  0.0 35.4 jit_solution(18305610442683366603)
XLA Ops:
  0.6 32.6 %shard_map.76 = (f32[16,16,128]{2,1,0:T(8,128)S(1)}, f32[3,8,16,256]{3,2,1,0:T(8,128)S(1)}, f32[3,8,16,256]{3,2,1,0:T(8,128)S(1)}) custom-call(f32[16,16,128]{2,1,0:T(8,128)} %kelvin.1, s32[16,16,128]{2,1,0:T(8,128)} %label.1, s32[16,16,128]{2,1,0:T(8,128)} %patch.1, f32[4,4]{1,0:T(4,128)} %traits_in.1, f32[16]{0:T(128)} %power_in.1), custom_call_target="tpu_custom_call" | custom-call | tf_op jit(solution)/shard_map/pallas_call | solution.py:800
  33.2 0.7 %copy.11 = f32[16,16,128]{2,1,0:T(8,128)} copy(f32[16,16,128]{2,1,0:T(8,128)S(1)} %get-tuple-element.6) | data formatting | bytes 262144
  33.9 0.7 %copy.12 = f32[3,8,16,256]{3,2,1,0:T(8,128)} copy(f32[3,8,16,256]{3,2,1,0:T(8,128)S(1)} %get-tuple-element.7) | data formatting | bytes 786432
  34.6 0.7 %copy.13 = f32[3,8,16,256]{3,2,1,0:T(8,128)} copy(f32[3,8,16,256]{3,2,1,0:T(8,128)S(1)} %get-tuple-element.8) | data formatting | bytes 786432

commit v3 on v2

--- a/solution.py
+++ b/solution.py
@@ -24,10 +24,6 @@
 def turn(f, amount):
     amount %= f.shape[-1]
     return pltpu.roll(f, amount, f.ndim - 1) if amount else f
-
-
-def both_lanes(f):
-    return turn(f, -1) + turn(f, 1)
 
 
 def three(ref, index, at):
@@ -76,30 +72,23 @@
     )
 
 
-def gradient_finish(out):
-    za, zb, xa, xb, yc = out
-    return za + both_lanes(zb), xa + both_lanes(xb), turn(yc, -1) - turn(yc, 1)
-
-
 def matrix_parts(f):
     p, s, d = f
-    a, b = p + 0.5 * s, p + (5.0 / 9.0) * s
-    q = p + s
+    after, before = turn(p, -1), turn(p, 1)
+    psum, pdiff = after + before, after - before
+    s_after, s_before = turn(s, -1), turn(s, 1)
+    ssum, sdiff = s_after + s_before, s_after - s_before
+    d_after, d_before = turn(d, -1), turn(d, 1)
+    dsum, ddiff = d_after + d_before, d_after - d_before
+    near, corner = s + psum, (5.0 / 9.0) * ssum
     return (
-        (2.0 * a + p, s, None), (b, a, None),
-        (q, 3.0 * s, None), (0.5 * p + (5.0 / 9.0) * s, q, None),
-        (a, s, None), (b, 2.0 * a + p, None),
-        (None, None, 0.5 * d), (None, None, (2.0 / 9.0) * d),
-        (None, None, a - 0.5 * b),
-        ((2.0 / 9.0) * d, 0.5 * d, None),
-    )
-
-
-def matrix_finish(out):
-    return (
-        out[0] + both_lanes(out[1]), out[2] + both_lanes(out[3]), out[4] + both_lanes(out[5]),
-        out[6] + both_lanes(out[7]), turn(out[8], -1) - turn(out[8], 1), turn(out[9], -1) - turn(out[9], 1),
-    )
+        (3.0 * p + near + corner, near + 0.5 * ssum, None),
+        (p + s + 0.5 * psum + corner, near + 2.0 * s + ssum, None),
+        (p + psum + 0.5 * s + corner, near + 2.0 * psum + ssum, None),
+        (None, None, 0.5 * d + (2.0 / 9.0) * dsum),
+        (None, None, 0.5 * pdiff + (2.0 / 9.0) * sdiff),
+        ((2.0 / 9.0) * ddiff, 0.5 * ddiff, None),
+    ), (after, before)
 
 
 def absorb(parts, held, below):
@@ -169,9 +158,9 @@
     warmed, solution, residual,
     traits, power_table, table_sem, vown, moment_s,
     temp, temp2, lab, pat, cond, rate_s, pow_s, gx_s, gy_s, gz_s,
-    mod, strain, both, mask, mats, v0, v1, v2, v3,
+    mod, strain, both, mask, mats, mod_beside, strain_beside, v0, v1, v2, v3,
     vrecv, late_src, late_got, pack_f, pack_i, got_f, got_i, red_src, red_buf,
-    local_sem, send_sem, recv_sem, vsend_sem, vrecv_sem, late_send, late_recv, rsend_sem, rrecv_sem,
+    local_sem, send_sem, recv_sem, vsend_sem, vrecv_sem, late_send, late_recv, round_sem, rsend_sem, rrecv_sem,
 ):
     nx, ny, nz = sizes
     v = (v0, v1, v2, v3)
@@ -213,13 +202,40 @@
 
     barrier = pltpu.get_barrier_semaphore()
 
-    def greet(k, _):
-        pl.semaphore_signal(
-            barrier, inc=1, device_id=coords(lax.rem(me + k, total)), device_id_type=MESH
+    def inside_mesh(dx, dc):
+        return jnp.logical_and(
+            jnp.logical_and(ix + dx >= 0, ix + dx < nx), jnp.logical_and(ic + dc >= 0, ic + dc < nc)
         )
-        return 0
-
-    lax.fori_loop(1, total, greet, 0, unroll=4)
+
+    def beside_of(dx, dc):
+        return coords(lax.rem(ix + dx + nx, nx) * nc + lax.rem(ic + dc + nc, nc))
+
+    def hail(semaphore, offsets):
+        for dx, dc in offsets:
+            @pl.when(inside_mesh(dx, dc))
+            def _(dx=dx, dc=dc):
+                pl.semaphore_signal(
+                    semaphore, inc=1, device_id=beside_of(dx, dc), device_id_type=MESH
+                )
+
+    def hear(semaphore, offsets):
+        count = sum(jnp.where(inside_mesh(dx, dc), 1, 0) for dx, dc in offsets)
+        pl.semaphore_wait(semaphore, count)
+
+    near = list(DIRECTIONS) + [(0, sign * step) for step in range(2, nz) for sign in (-1, 1)]
+    hail(barrier, near)
+    rounds = []
+    for extent, axis in ((nc, 1), (nx, 0)):
+        reach = 1
+        while reach < extent - 1:
+            rounds.append([(0, sign * reach) if axis else (sign * reach, 0) for sign in (-1, 1)])
+            reach *= 2
+
+    def pass_on(number):
+        if 0 < number <= len(rounds):
+            hear(round_sem.at[number - 1], rounds[number - 1])
+        if number < len(rounds):
+            hail(round_sem.at[number], rounds[number])
 
     own = (slice(1, layers + 1), slice(8, 8 + rows))
     local = [
@@ -237,13 +253,7 @@
 
     def transfers(number):
         dx, dc = DIRECTIONS[number]
-        there = (lax.rem(ix + dx + nx, nx) * nc) + lax.rem(ic + dc + nc, nc)
-        target = jnp.logical_and(
-            jnp.logical_and(ix + dx >= 0, ix + dx < nx), jnp.logical_and(ic + dc >= 0, ic + dc < nc)
-        )
-        origin = jnp.logical_and(
-            jnp.logical_and(ix - dx >= 0, ix - dx < nx), jnp.logical_and(ic - dc >= 0, ic - dc < nc)
-        )
+        target, origin = inside_mesh(dx, dc), inside_mesh(-dx, -dc)
         if dx == 0:
             from_rows, to_rows = pl.ds(0, rows), pl.ds(0, rows)
         elif dx == 1:
@@ -263,7 +273,7 @@
         copies = [
             pltpu.make_async_remote_copy(
                 src_ref=a, dst_ref=b, send_sem=send_sem.at[number, i],
-                recv_sem=recv_sem.at[number, i], device_id=coords(there), device_id_type=MESH,
+                recv_sem=recv_sem.at[number, i], device_id=beside_of(dx, dc), device_id_type=MESH,
             )
             for i, (a, b) in enumerate(pairs)
         ]
@@ -284,7 +294,7 @@
             else:
                 pack_i[side, index - 1] = packed
 
-    pl.semaphore_wait(barrier, total - 1)
+    hear(barrier, near)
     for wanted in (True, False):
         for target, _, copies, dc in moves:
             if (dc == 0) != wanted:
@@ -387,6 +397,7 @@
         for ref, values in zip((mod, strain, mask), zip(*kept)):
             to_ring(ref, p, chunk_list[0], values)
 
+    pass_on(0)
     own_list, halo_list = range(own_chunks), range(own_chunks, heat_chunks)
     over(main, lambda p: prepare(p, own_list), 4)
     for chunk in own_list:
@@ -397,6 +408,7 @@
             for copy in copies:
                 copy.wait_recv()
 
+    pass_on(1)
     for chunk in own_list:
         outer_strip(chunk)
     for chunk in halo_list:
@@ -481,6 +493,8 @@
     for ref in (strain, both):
         wrap(ref, ())
 
+    pass_on(2)
+
     def mended(ref, index, z, t, g, chunk):
         here = slice(at(chunk), at(chunk) + 8)
         return patched(ref[(*index, 1 + z, here)], ref[(*index, first_tile + t, here)], g)
@@ -506,13 +520,26 @@
                 lambda p, out, chunk=chunk: emit(p, chunk, out),
             )
 
+    def matrix_planes(p, where):
+        parts, beside = matrix_parts(three(mod, (p,), where))
+        if not isinstance(p, int) or p in strips or p in main:
+            for side, value in enumerate(beside):
+                mod_beside[side, p, where - 8 : where] = value
+        return parts
+
     def matrix_emit(p, chunk, out):
         here = slice(at(chunk), at(chunk) + 8)
         diagonal = (4.0 * (ANCHOR + K_TOTAL)) * mod[p, here] - 1.0
-        for c, value in enumerate(matrix_finish(out)):
+        for c, value in enumerate(out):
             mats[c, p, 8 * chunk : 8 * chunk + 8] = value + diagonal if c < 3 else value
 
-    sweep(range(chunks), lambda p, where: matrix_parts(three(mod, (p,), where)), matrix_emit, layers - 1)
+    sweep(range(chunks), matrix_planes, matrix_emit, layers - 1)
+
+    for p in (*main, *strips):
+        for chunk in range(chunks):
+            here = slice(at(chunk), at(chunk) + 8)
+            for side in (0, 1):
+                strain_beside[side, p, 8 * chunk : 8 * chunk + 8] = turn(strain[p, here], 2 * side - 1)
 
     def load_parts(p, where):
         return tuple(a for ref in (strain, mod, both) for a in gradient_parts(three(ref, (p,), where)))
@@ -525,9 +552,20 @@
     def load_emit(p, chunk, out):
         here = slice(at(chunk), at(chunk) + 8)
         m, s, inside = mod[p, here], strain[p, here], mask[p, here]
-        found = [gradient_finish(out[5 * i : 5 * i + 5]) for i in range(3)]
+        m_after, m_before = (mod_beside[side, p, 8 * chunk : 8 * chunk + 8] for side in (0, 1))
+        s_after, s_before = (strain_beside[side, p, 8 * chunk : 8 * chunk + 8] for side in (0, 1))
+        of_s, of_m, of_both = out[:5], out[5:10], out[10:]
+
+        def joined(i, m, s):
+            return m * of_s[i] + s * of_m[i] + of_both[i]
+
+        def beside(i):
+            return turn(joined(i, m_before, s_before), -1), turn(joined(i, m_after, s_after), 1)
+
+        (z_up, z_down), (x_up, x_down), (y_up, y_down) = beside(1), beside(3), beside(4)
+        found = (joined(0, m, s) + z_up + z_down, joined(2, m, s) + x_up + x_down, y_up - y_down)
         for c in range(3):
-            value = -inside * (m * found[0][c] + s * found[1][c] + found[2][c])
+            value = -inside * found[c]
             keep_basis(0, p, chunk, c, value)
 
     sweep(range(chunks), load_parts, load_emit, layers - 1)
@@ -570,6 +608,7 @@
 
     moment_s[0] = mend(settle(0, True), (None, empty))[1]
     share_basis(0)
+    pass_on(3)
 
     def apply(k, chunk_list):
         def parts(p, where):
@@ -607,6 +646,9 @@
 
     for k in range(ITERS - 1):
         grow(k, 0)
+        pass_on(4 + k)
+    for number in range(4 + ITERS - 1, len(rounds) + 1):
+        pass_on(number)
     apply(ITERS - 1, range(own_chunks))
     odd, even = mend(settle(ITERS, False), (empty, empty))
     moment_s[2 * ITERS - 1] = odd
@@ -809,7 +851,7 @@
             vmem(heated, f32), vmem(heated, f32), vmem(heated, i32), vmem(heated, i32),
             *[vmem(heated, f32)] * 6,
             *[vmem(kept, f32)] * 4,
-            vmem((6, planes, rows + 8, cols), f32),
+            vmem((6, planes, rows + 8, cols), f32), *[vmem((2, planes, rows + 8, cols), f32)] * 2,
             *[vmem((6, *kept), f32)] * ITERS, vmem((3, *kept), f32),
             vmem((ITERS + 1, nz - 1, 3, early, rows, cols), f32),
             vmem(late, f32), vmem(late, f32),
@@ -818,7 +860,8 @@
             vmem((1, cols), f32), vmem((total, 1, cols), f32),
             dma((3,)), dma((8, 3)), dma((8, 3)),
             dma((ITERS + 1, nz - 1)), dma((ITERS + 1, nz - 1)),
-            dma((nz - 1, 2)), dma((nz - 1, 2)), dma((total,)), dma((total,)),
+            dma((nz - 1, 2)), dma((nz - 1, 2)),
+            pltpu.SemaphoreType.REGULAR((2 * max(nx, ny * nz).bit_length(),)), dma((total,)), dma((total,)),
         ],
         compiler_params=pltpu.CompilerParams(
             collective_id=0, has_side_effects=True, vmem_limit_bytes=48 * 1024 * 1024

time: 35.5 us -> 34.2 us (0.963)
  Pallas kernels: 32.6 us -> 31.2 us
    pallas_call x1, Pallas kernels: 32.6 us -> 31.2 us  [per_device(): pl.pallas_call(functools.partial(kernel, sizes), out_shape=shapes, in_spe...]
where the time goes in v3:
time: 34.2 us; the launch traced here: 34 us
  Pallas kernels  31.2 us (91%)
  local copies, waits for them, and re-layouts  2.15 us (6%)
  between operations  0.64 us (2%)
    pallas_call x1, Pallas kernels, per_device(): pl.pallas_call(functools.partial(kernel, sizes), out_shape=shapes, in_spe...  31.2 us
    unnamed x3, local copies, waits for them, and re-layouts  2.15 us

profile of v3, /device:TPU:0, one launch (start us, length us, event | category | flops | bytes accessed | tf_op | source)
XLA Modules:
  0.0 34.0 jit_solution(7866480822531734255)
XLA Ops:
  0.6 31.2 %shard_map.76 = (f32[16,16,128]{2,1,0:T(8,128)S(1)}, f32[3,8,16,256]{3,2,1,0:T(8,128)S(1)}, f32[3,8,16,256]{3,2,1,0:T(8,128)S(1)}) custom-call(f32[16,16,128]{2,1,0:T(8,128)} %kelvin.1, s32[16,16,128]{2,1,0:T(8,128)} %label.1, s32[16,16,128]{2,1,0:T(8,128)} %patch.1, f32[4,4]{1,0:T(4,128)} %traits_in.1, f32[16]{0:T(128)} %power_in.1), custom_call_target="tpu_custom_call" | custom-call | tf_op jit(solution)/shard_map/pallas_call | solution.py:842
  31.9 0.7 %copy.11 = f32[16,16,128]{2,1,0:T(8,128)} copy(f32[16,16,128]{2,1,0:T(8,128)S(1)} %get-tuple-element.6) | data formatting | bytes 262144
  32.5 0.7 %copy.12 = f32[3,8,16,256]{3,2,1,0:T(8,128)} copy(f32[3,8,16,256]{3,2,1,0:T(8,128)S(1)} %get-tuple-element.7) | data formatting | bytes 786432
  33.3 0.7 %copy.13 = f32[3,8,16,256]{3,2,1,0:T(8,128)} copy(f32[3,8,16,256]{3,2,1,0:T(8,128)S(1)} %get-tuple-element.8) | data formatting | bytes 786432

commit v4 on v3

--- a/solution.py
+++ b/solution.py
@@ -11,7 +11,7 @@
 HALO = 8
 REACH = 6
 EDGE = 4
-EARLY = 4
+EARLY = 5
 STRIP = 16
 PAIR = 2 * STRIP
 TIME_STEP = 0.03
@@ -662,35 +662,29 @@
     red_src[...] = row
     red_buf[me] = row
 
-    def spread(k):
-        there = lax.rem(me + k, total)
+    def placed(offset):
+        a, rest = offset // nc, offset % nc
+        found = []
+        for here, step, size in ((ix, a, nx), (iy, rest // nz, ny), (iz, rest % nz, nz)):
+            there = here + step
+            found.append(jnp.where(there >= size, there - size, there) if step else here)
+        return tuple(found)
+
+    def spread(offset):
         return pltpu.make_async_remote_copy(
-            src_ref=red_src, dst_ref=red_buf.at[me], send_sem=rsend_sem.at[k],
-            recv_sem=rrecv_sem.at[k], device_id=coords(there), device_id_type=MESH,
+            src_ref=red_src, dst_ref=red_buf.at[me], send_sem=rsend_sem.at[0],
+            recv_sem=rrecv_sem.at[0], device_id=placed(offset), device_id_type=MESH,
         )
 
-    def collect(k):
-        there = lax.rem(me + total - k, total)
-        return pltpu.make_async_remote_copy(
-            src_ref=red_src, dst_ref=red_buf.at[there], send_sem=rsend_sem.at[k],
-            recv_sem=rrecv_sem.at[k], device_id=coords(there), device_id_type=MESH,
-        )
-
-    def start(k, _):
-        spread(k).start()
-        return 0
-
-    def finish(k, _):
-        collect(k).wait_recv()
-        return 0
-
-    def sent(k, _):
-        spread(k).wait_send()
-        return 0
-
-    lax.fori_loop(1, total, start, 0, unroll=4)
+    everyone = pltpu.make_async_remote_copy(
+        src_ref=red_buf.at[0 : total - 1], dst_ref=red_buf.at[0 : total - 1],
+        send_sem=rsend_sem.at[0], recv_sem=rrecv_sem.at[0],
+        device_id=placed(1), device_id_type=MESH,
+    )
+    for offset in sorted(range(1, total), key=lambda k: -min(k % nc, nc - k % nc)):
+        spread(offset).start()
     share_basis(ITERS)
-    lax.fori_loop(1, total, finish, 0, unroll=4)
+    everyone.wait_recv()
 
     def add(k, acc):
         return acc + red_buf[k]
@@ -820,7 +814,7 @@
             copy.wait_send()
     for copy in late_copies:
         copy.wait_send()
-    lax.fori_loop(1, total, sent, 0, unroll=4)
+    everyone.wait_send()
 
 
 def per_device(sizes, *arrays):
@@ -861,7 +855,7 @@
             dma((3,)), dma((8, 3)), dma((8, 3)),
             dma((ITERS + 1, nz - 1)), dma((ITERS + 1, nz - 1)),
             dma((nz - 1, 2)), dma((nz - 1, 2)),
-            pltpu.SemaphoreType.REGULAR((2 * max(nx, ny * nz).bit_length(),)), dma((total,)), dma((total,)),
+            pltpu.SemaphoreType.REGULAR((2 * max(nx, ny * nz).bit_length(),)), dma((1,)), dma((1,)),
         ],
         compiler_params=pltpu.CompilerParams(
             collective_id=0, has_side_effects=True, vmem_limit_bytes=48 * 1024 * 1024

time: 34.2 us -> 32.4 us (0.947)
  Pallas kernels: 31.2 us -> 29.5 us
    pallas_call x1, Pallas kernels: 31.2 us -> 29.5 us  [per_device(): pl.pallas_call(functools.partial(kernel, sizes), out_shape=shapes, in_spe...]
where the time goes in v4:
time: 32.4 us; the launch traced here: 32.3 us
  Pallas kernels  29.5 us (91%)
  local copies, waits for them, and re-layouts  2.15 us (7%)
  between operations  0.64 us (2%)
    pallas_call x1, Pallas kernels, per_device(): pl.pallas_call(functools.partial(kernel, sizes), out_shape=shapes, in_spe...  29.5 us
    unnamed x3, local copies, waits for them, and re-layouts  2.15 us

profile of v4, /device:TPU:0, one launch (start us, length us, event | category | flops | bytes accessed | tf_op | source)
XLA Modules:
  0.0 32.3 jit_solution(17575460009582859510)
XLA Ops:
  0.6 29.5 %shard_map.76 = (f32[16,16,128]{2,1,0:T(8,128)S(1)}, f32[3,8,16,256]{3,2,1,0:T(8,128)S(1)}, f32[3,8,16,256]{3,2,1,0:T(8,128)S(1)}) custom-call(f32[16,16,128]{2,1,0:T(8,128)} %kelvin.1, s32[16,16,128]{2,1,0:T(8,128)} %label.1, s32[16,16,128]{2,1,0:T(8,128)} %patch.1, f32[4,4]{1,0:T(4,128)} %traits_in.1, f32[16]{0:T(128)} %power_in.1), custom_call_target="tpu_custom_call" | custom-call | tf_op jit(solution)/shard_map/pallas_call | solution.py:836
  30.1 0.7 %copy.11 = f32[16,16,128]{2,1,0:T(8,128)} copy(f32[16,16,128]{2,1,0:T(8,128)S(1)} %get-tuple-element.6) | data formatting | bytes 262144
  30.8 0.7 %copy.12 = f32[3,8,16,256]{3,2,1,0:T(8,128)} copy(f32[3,8,16,256]{3,2,1,0:T(8,128)S(1)} %get-tuple-element.7) | data formatting | bytes 786432
  31.5 0.7 %copy.13 = f32[3,8,16,256]{3,2,1,0:T(8,128)} copy(f32[3,8,16,256]{3,2,1,0:T(8,128)S(1)} %get-tuple-element.8) | data formatting | bytes 786432

commit v5 on v4

--- a/solution.py
+++ b/solution.py
@@ -112,7 +112,7 @@
     return [-h if side is None else h for (side, _, _), h in zip(kinds, held)]
 
 
-def stream_closed(first, count, parts, emit, unroll):
+def stream_closed(first, count, parts, emit):
     kinds = parts(first)
     zero = jnp.zeros_like(next(c for _, c, _ in kinds if c is not None))
     held = [zero if side is None else centre for side, centre, _ in kinds]
@@ -120,12 +120,9 @@
         diff if side is None else (side if diff is None else side - diff) for side, _, diff in kinds
     ]
 
-    def body(p, carry):
-        out, held, below = absorb(parts(p), *carry)
+    for p in range(first + 1, first + count):
+        out, held, below = absorb(parts(p), held, below)
         emit(p - 1, out)
-        return held, below
-
-    held, below = lax.fori_loop(first + 1, first + count, body, (held, below), unroll=unroll)
     emit(first + count - 1, closing(kinds, held))
 
 
@@ -495,30 +492,24 @@
 
     pass_on(2)
 
-    def mended(ref, index, z, t, g, chunk):
-        here = slice(at(chunk), at(chunk) + 8)
-        return patched(ref[(*index, 1 + z, here)], ref[(*index, first_tile + t, here)], g)
-
-    def mend(body, carry):
-        for g in range(groups):
-            def step(t, carry, g=g):
-                for chunk in range(own_chunks):
-                    carry = body(tiles * g + t, t, g, chunk, carry)
-                return carry
-
-            carry = lax.fori_loop(0, tiles, step, carry, unroll=tiles)
-        return carry
-
-    def sweep(chunk_list, parts, emit, unroll):
+    def settle(k, p, chunk, c, value, sums):
+        if chunk >= own_chunks or p not in main:
+            return
+        z, rows_here = p - 1, slice(8 * chunk, 8 * chunk + 8)
+        edge = v[k][c, first_tile + z % tiles, at(chunk) : at(chunk) + 8]
+        value = patched(value, edge, z // tiles)
+        vown[k, c, z, rows_here] = value
+        sums[1] = sums[1] + value * value
+        if k > 0:
+            sums[0] = sums[0] + value * vown[k - 1, c, z, rows_here]
+
+    def sweep(chunk_list, parts, emit):
         for chunk in chunk_list:
-            stream_closed(
-                1, layers, lambda p, chunk=chunk: parts(p, at(chunk)),
-                lambda p, out, chunk=chunk: emit(p, chunk, out), unroll,
-            )
-            stream_open(
-                first_tile, tiles, lambda p, chunk=chunk: parts(p, at(chunk)),
-                lambda p, out, chunk=chunk: emit(p, chunk, out),
-            )
+            for run, first, count in ((stream_open, first_tile, tiles), (stream_closed, 1, layers)):
+                run(
+                    first, count, lambda p, chunk=chunk: parts(p, at(chunk)),
+                    lambda p, out, chunk=chunk: emit(p, chunk, out),
+                )
 
     def matrix_planes(p, where):
         parts, beside = matrix_parts(three(mod, (p,), where))
@@ -533,7 +524,7 @@
         for c, value in enumerate(out):
             mats[c, p, 8 * chunk : 8 * chunk + 8] = value + diagonal if c < 3 else value
 
-    sweep(range(chunks), matrix_planes, matrix_emit, layers - 1)
+    sweep(range(chunks), matrix_planes, matrix_emit)
 
     for p in (*main, *strips):
         for chunk in range(chunks):
@@ -567,26 +558,7 @@
         for c in range(3):
             value = -inside * found[c]
             keep_basis(0, p, chunk, c, value)
-
-    sweep(range(chunks), load_parts, load_emit, layers - 1)
-
-    def settle(k, more):
-        if more:
-            for c in range(6):
-                wrap(v[k], (c,))
-
-        def body(z, t, g, chunk, carry):
-            odd, even = carry
-            rows_here = slice(8 * chunk, 8 * chunk + 8)
-            for c in range(3):
-                value = mended(v[k], (c,), z, t, g, chunk)
-                vown[k, c, z, rows_here] = value
-                even = even + value * value
-                if odd is not None:
-                    odd = odd + value * vown[k - 1, c, z, rows_here]
-            return odd, even
-
-        return body
+            settle(0, p, chunk, c, value, sums)
 
     def shares(k):
         found = []
@@ -606,11 +578,19 @@
         for copy in shares(k):
             copy.start()
 
-    moment_s[0] = mend(settle(0, True), (None, empty))[1]
+    def wrap_basis(k):
+        for c in range(6):
+            wrap(v[k], (c,))
+
+    sums = [empty, empty]
+    sweep(range(own_chunks), load_parts, load_emit)
+    moment_s[0] = sums[1]
     share_basis(0)
+    sweep(range(own_chunks, chunks), load_parts, load_emit)
+    wrap_basis(0)
     pass_on(3)
 
-    def apply(k, chunk_list):
+    def apply(k, chunk_list, sums):
         def parts(p, where):
             return operator_parts(*[three(v[k], (c, p), where) for c in range(3)]) + operator_parts(
                 *[three(v[k], (3 + c, p), where) for c in range(3)]
@@ -629,30 +609,26 @@
             first, second = operator_finish(out[:9]), operator_finish(out[9:])
             for c in range(3):
                 value = grown[c] - m * first[c] - second[c]
-                if len(chunk_list) > own_chunks:
-                    keep_basis(k + 1, p, chunk, c, inside * value)
-                else:
+                if k + 1 < ITERS:
+                    value = inside * value
+                    keep_basis(k + 1, p, chunk, c, value)
+                elif p in strips:
                     v[k + 1][c, p, here] = value
-
-        sweep(chunk_list, parts, emit, layers - 1)
-
-    def grow(k, _):
-        apply(k, range(chunks))
-        odd, even = mend(settle(k + 1, True), (empty, empty))
-        moment_s[2 * k + 1] = odd
-        moment_s[2 * k + 2] = even
-        share_basis(k + 1)
-        return 0
-
-    for k in range(ITERS - 1):
-        grow(k, 0)
-        pass_on(4 + k)
+                settle(k + 1, p, chunk, c, value, sums)
+
+        sweep(chunk_list, parts, emit)
+
+    for k in range(ITERS):
+        sums = [empty, empty]
+        apply(k, range(own_chunks), sums)
+        moment_s[2 * k + 1], moment_s[2 * k + 2] = sums
+        if k + 1 < ITERS:
+            share_basis(k + 1)
+            apply(k, range(own_chunks, chunks), sums)
+            wrap_basis(k + 1)
+            pass_on(4 + k)
     for number in range(4 + ITERS - 1, len(rounds) + 1):
         pass_on(number)
-    apply(ITERS - 1, range(own_chunks))
-    odd, even = mend(settle(ITERS, False), (empty, empty))
-    moment_s[2 * ITERS - 1] = odd
-    moment_s[2 * ITERS] = even
 
     lane8 = lax.broadcasted_iota(jnp.int32, (1, cols), 1)
     row = jnp.zeros((1, cols), jnp.float32)
@@ -684,7 +660,15 @@
     for offset in sorted(range(1, total), key=lambda k: -min(k % nc, nc - k % nc)):
         spread(offset).start()
     share_basis(ITERS)
+    for target, _, copies, _ in moves:
+        @pl.when(target)
+        def _(copies=copies):
+            for copy in copies:
+                copy.wait_send()
+    for copy in shares(0):
+        copy.wait_send()
     everyone.wait_recv()
+    everyone.wait_send()
 
     def add(k, acc):
         return acc + red_buf[k]
@@ -804,17 +788,11 @@
                     for here in row_tiles:
                         target[c, early + z, here, lanes_of(step)] = late_got[step - 1, part, c, z, here]
 
-    for target, _, copies, _ in moves:
-        @pl.when(target)
-        def _(copies=copies):
-            for copy in copies:
-                copy.wait_send()
-    for k in range(ITERS + 1):
+    for k in range(1, ITERS + 1):
         for copy in shares(k):
             copy.wait_send()
     for copy in late_copies:
         copy.wait_send()
-    everyone.wait_send()
 
 
 def per_device(sizes, *arrays):

time: 32.4 us -> 32.1 us (level)
  Pallas kernels: 29.5 us -> 29.1 us
    pallas_call x1, Pallas kernels: 29.5 us -> 29.1 us  [per_device(): pl.pallas_call(functools.partial(kernel, sizes), out_shape=shapes, in_spe...]
where the time goes in v5:
time: 32.1 us; the launch traced here: 31.9 us
  Pallas kernels  29.1 us (91%)
  local copies, waits for them, and re-layouts  2.15 us (7%)
  between operations  0.64 us (2%)
    pallas_call x1, Pallas kernels, per_device(): pl.pallas_call(functools.partial(kernel, sizes), out_shape=shapes, in_spe...  29.1 us
    unnamed x3, local copies, waits for them, and re-layouts  2.15 us

profile of v5, /device:TPU:0, one launch (start us, length us, event | category | flops | bytes accessed | tf_op | source)
XLA Modules:
  0.0 31.9 jit_solution(16392150926066304250)
XLA Ops:
  0.6 29.1 %shard_map.76 = (f32[16,16,128]{2,1,0:T(8,128)S(1)}, f32[3,8,16,256]{3,2,1,0:T(8,128)S(1)}, f32[3,8,16,256]{3,2,1,0:T(8,128)S(1)}) custom-call(f32[16,16,128]{2,1,0:T(8,128)} %kelvin.1, s32[16,16,128]{2,1,0:T(8,128)} %label.1, s32[16,16,128]{2,1,0:T(8,128)} %patch.1, f32[4,4]{1,0:T(4,128)} %traits_in.1, f32[16]{0:T(128)} %power_in.1), custom_call_target="tpu_custom_call" | custom-call | tf_op jit(solution)/shard_map/pallas_call | solution.py:814
  29.8 0.7 %copy.11 = f32[16,16,128]{2,1,0:T(8,128)} copy(f32[16,16,128]{2,1,0:T(8,128)S(1)} %get-tuple-element.6) | data formatting | bytes 262144
  30.4 0.7 %copy.12 = f32[3,8,16,256]{3,2,1,0:T(8,128)} copy(f32[3,8,16,256]{3,2,1,0:T(8,128)S(1)} %get-tuple-element.7) | data formatting | bytes 786432
  31.2 0.7 %copy.13 = f32[3,8,16,256]{3,2,1,0:T(8,128)} copy(f32[3,8,16,256]{3,2,1,0:T(8,128)S(1)} %get-tuple-element.8) | data formatting | bytes 786432

commit v6 on v5

--- a/solution.py
+++ b/solution.py
@@ -665,8 +665,9 @@
         def _(copies=copies):
             for copy in copies:
                 copy.wait_send()
-    for copy in shares(0):
-        copy.wait_send()
+    for k in range(ITERS):
+        for copy in shares(k):
+            copy.wait_send()
     everyone.wait_recv()
     everyone.wait_send()
 
@@ -788,10 +789,7 @@
                     for here in row_tiles:
                         target[c, early + z, here, lanes_of(step)] = late_got[step - 1, part, c, z, here]
 
-    for k in range(1, ITERS + 1):
-        for copy in shares(k):
-            copy.wait_send()
-    for copy in late_copies:
+    for copy in shares(ITERS) + late_copies:
         copy.wait_send()
 
 

time: 32.1 us -> 32.1 us (level)
  no operation moved by 1% of the time
where the time goes in v6:
time: 32.1 us; the launch traced here: 31.9 us
  Pallas kernels  29.1 us (91%)
  local copies, waits for them, and re-layouts  2.15 us (7%)
  between operations  0.64 us (2%)
    pallas_call x1, Pallas kernels, per_device(): pl.pallas_call(functools.partial(kernel, sizes), out_shape=shapes, in_spe...  29.1 us
    unnamed x3, local copies, waits for them, and re-layouts  2.15 us

profile of v6, /device:TPU:0, one launch (start us, length us, event | category | flops | bytes accessed | tf_op | source)
XLA Modules:
  0.0 31.9 jit_solution(7429827972076132180)
XLA Ops:
  0.6 29.1 %shard_map.76 = (f32[16,16,128]{2,1,0:T(8,128)S(1)}, f32[3,8,16,256]{3,2,1,0:T(8,128)S(1)}, f32[3,8,16,256]{3,2,1,0:T(8,128)S(1)}) custom-call(f32[16,16,128]{2,1,0:T(8,128)} %kelvin.1, s32[16,16,128]{2,1,0:T(8,128)} %label.1, s32[16,16,128]{2,1,0:T(8,128)} %patch.1, f32[4,4]{1,0:T(4,128)} %traits_in.1, f32[16]{0:T(128)} %power_in.1), custom_call_target="tpu_custom_call" | custom-call | tf_op jit(solution)/shard_map/pallas_call | solution.py:812
  29.8 0.7 %copy.11 = f32[16,16,128]{2,1,0:T(8,128)} copy(f32[16,16,128]{2,1,0:T(8,128)S(1)} %get-tuple-element.6) | data formatting | bytes 262144
  30.4 0.7 %copy.12 = f32[3,8,16,256]{3,2,1,0:T(8,128)} copy(f32[3,8,16,256]{3,2,1,0:T(8,128)S(1)} %get-tuple-element.7) | data formatting | bytes 786432
  31.2 0.7 %copy.13 = f32[3,8,16,256]{3,2,1,0:T(8,128)} copy(f32[3,8,16,256]{3,2,1,0:T(8,128)S(1)} %get-tuple-element.8) | data formatting | bytes 786432
